TPU v7x, 512 devices: a whole 4x8x8 slice. The times are simulated.
512 devices in a mesh: row: 64 (over z, y_lo, x), ch: 8 (over y_hi, core).
Axes of the slice: x: 4, y: 8 (y_hi: 4, y_lo: 2; y = y_hi * 2 + y_lo), z: 8, core: 2. Of those that a mesh axis runs over, the one named last changes fastest.
Arguments:
- pair_rep: float32 [1024, 1024, 128], P('row', 'ch'), may hold values from -6 to 6
- residue_mask: int32 [1024], replicated, may hold values 0 or 1
- pair_gain: float32 [2, 128], replicated, may hold values from 0.5 to 1.5
- pair_shift: float32 [2, 128], replicated, may hold values from -3 to 3
- panel_weight: bfloat16 [2, 128, 512], replicated, may hold values from -0.5 to 0.5
- panel_bias: float32 [2, 512], replicated, may hold values from -3 to 3
- gate_weight: bfloat16 [2, 128, 128], replicated, may hold values from -0.5 to 0.5
- gate_bias: float32 [2, 128], replicated, may hold values from -3 to 3
- hidden_gain: float32 [2, 128], replicated, may hold values from 0.5 to 1.5
- hidden_shift: float32 [2, 128], replicated, may hold values from -3 to 3
- output_weight: bfloat16 [2, 128, 128], replicated, may hold values from -0.5 to 0.5
- output_bias: float32 [2, 128], replicated, may hold values from -3 to 3
Outputs:
- updated_pair: float32 [1024, 1024, 128], P('row', 'ch')
All inputs are finite; a program needn't handle non-finite values.
Results may differ from a plain program's by a relative error of at most 0.0039.
Values may be sent and summed in bfloat16 or wider, within the bound.
A program may use at most 64 MiB of HBM per device.

v0:
```python
import jax
import jax.numpy as jnp
from jax import lax
from jax.sharding import PartitionSpec as P

PAIR_EPSILON = 1e-05
HIDDEN_EPSILON = 1.0


def layer_norm(values, gain_value, shift_value, along, epsilon):
    center = jnp.mean(values, axis=along, keepdims=True)
    offset = values - center
    spread = jnp.mean(offset * offset, axis=along, keepdims=True)
    return offset * lax.rsqrt(spread + epsilon) * gain_value + shift_value


def project(
    current,
    cell_mask,
    section_index,
    pair_gain,
    pair_shift,
    panel_weight,
    panel_bias,
    gate_weight,
    gate_bias,
):
    normed = layer_norm(
        current, pair_gain[section_index], pair_shift[section_index], 2, PAIR_EPSILON
    ).astype(jnp.bfloat16)
    hidden_width = panel_weight.shape[2] // 4
    features = jnp.einsum(
        "rjc,cf->frj", normed, panel_weight[section_index], preferred_element_type=jnp.float32
    )
    features = features + panel_bias[section_index][:, None, None]
    left_panel = (
        cell_mask
        * jax.nn.sigmoid(features[:hidden_width])
        * features[hidden_width : 2 * hidden_width]
    ).astype(jnp.bfloat16)
    right_panel = (
        cell_mask
        * jax.nn.sigmoid(features[2 * hidden_width : 3 * hidden_width])
        * features[3 * hidden_width :]
    ).astype(jnp.bfloat16)
    gate_value = jax.nn.sigmoid(
        jnp.einsum(
            "rjc,cd->rjd", normed, gate_weight[section_index], preferred_element_type=jnp.float32
        )
        + gate_bias[section_index]
    )
    return (left_panel, right_panel, gate_value)


def local(
    pair_rep,
    residue_mask,
    pair_gain,
    pair_shift,
    panel_weight,
    panel_bias,
    gate_weight,
    gate_bias,
    hidden_gain,
    hidden_shift,
    output_weight,
    output_bias,
):
    row_count = pair_rep.shape[0]
    col_count = pair_rep.shape[1]
    hidden_width = panel_weight.shape[2] // 4
    row_total = lax.axis_size("row")
    col_total = lax.axis_size("ch")
    group = hidden_width // col_total
    per_slot = 1
    quarters = row_total // group
    slots = row_total // quarters
    sub_rows = row_count // quarters
    blocks = col_count // row_count
    row_index = lax.axis_index("row")
    col_index = lax.axis_index("ch")
    residue_float = residue_mask.astype(jnp.float32)
    row_mask = lax.dynamic_slice_in_dim(residue_float, row_index * row_count, row_count)
    col_mask = lax.dynamic_slice_in_dim(residue_float, col_index * col_count, col_count)
    cell_mask = row_mask[:, None] * col_mask[None, :]
    current = pair_rep
    for section_index in range(2):
        left_panel, right_panel, gate_value = project(
            current,
            cell_mask,
            section_index,
            pair_gain,
            pair_shift,
            panel_weight,
            panel_bias,
            gate_weight,
            gate_bias,
        )
        if section_index == 0:
            send_left = left_panel.reshape(
                col_total, slots, per_slot, quarters, sub_rows, col_count
            )
            send_left = jnp.transpose(send_left, (0, 1, 3, 2, 4, 5)).reshape(
                col_total, row_total, per_slot, sub_rows, col_count
            )
        else:
            send_left = left_panel.reshape(
                col_total, slots, per_slot, row_count, blocks, quarters, sub_rows
            )
            send_left = jnp.transpose(send_left, (0, 1, 5, 2, 3, 4, 6)).reshape(
                col_total, row_total, per_slot, row_count, blocks * sub_rows
            )
        send_right = right_panel.reshape(col_total, slots, 1, per_slot, row_count, col_count)
        send_right = jnp.broadcast_to(
            send_right, (col_total, slots, quarters, per_slot, row_count, col_count)
        ).reshape(col_total, row_total, per_slot, row_count, col_count)
        got_left, got_right = (
            lax.all_to_all(
                lax.all_to_all(send_left, "ch", split_axis=0, concat_axis=4, tiled=True),
                "row",
                split_axis=1,
                concat_axis=3,
                tiled=True,
            ),
            lax.all_to_all(
                lax.all_to_all(send_right, "ch", split_axis=0, concat_axis=4, tiled=True),
                "row",
                split_axis=1,
                concat_axis=3,
                tiled=True,
            ),
        )
        got_left = got_left[0, 0]
        got_right = got_right[0, 0]
        if section_index == 0:
            products = jnp.einsum(
                "hik,hjk->hij", got_left, got_right, preferred_element_type=jnp.float32
            )
        else:
            products = jnp.einsum(
                "hki,hkj->hij", got_left, got_right, preferred_element_type=jnp.float32
            )
        returned = products.reshape(per_slot, row_total, sub_rows, col_total, col_count)
        gathered = lax.all_to_all(
            lax.all_to_all(
                returned.astype(jnp.bfloat16), "row", split_axis=1, concat_axis=0, tiled=True
            ),
            "ch",
            split_axis=3,
            concat_axis=0,
            tiled=True,
        ).astype(returned.dtype)
        gathered = gathered.reshape(col_total, slots, quarters, per_slot, sub_rows, col_count)
        gathered = jnp.transpose(gathered, (0, 1, 3, 2, 4, 5)).reshape(
            hidden_width, row_count, col_count
        )
        normed = layer_norm(
            gathered,
            hidden_gain[section_index][:, None, None],
            hidden_shift[section_index][:, None, None],
            0,
            HIDDEN_EPSILON,
        ).astype(jnp.bfloat16)
        projected = jnp.einsum(
            "hrj,hc->rjc", normed, output_weight[section_index], preferred_element_type=jnp.float32
        )
        current = current + gate_value * (projected + output_bias[section_index])
    return current


def solution(mesh):
    return jax.shard_map(
        local,
        mesh=mesh,
        in_specs=(P("row", "ch", None), P(), P(), P(), P(), P(), P(), P(), P(), P(), P(), P()),
        out_specs=P("row", "ch", None),
        check_vma=False,
    )
```

profile of v0, /device:TPU:1, one launch (start us, length us, event | category | flops | bytes accessed | tf_op | source)
XLA Modules:
  0.0 462.9 jit_solution(5443563104782265272)
XLA Ops:
  0.0 0.8 convert_element_type.102
  1.0 1.6 reduce_sum.72
  2.6 1.9 multiply_reduce_fusion.3
  4.6 0.8 add_bitcast_fusion.1
  5.4 0.6 fusion.29
  6.0 1.2 copy.134
  7.2 10.2 %all-to-all-start = ((bf16[8,64,1,4,128]{4,3,1,2,0:T(4,128)(2,1)}), bf16[8,64,1,4,128]{4,3,1,2,0:T(4,128)(2,1)S(1)}, u32[]{:S(2)}, u32[]{:S(2)}) async-start(bf16[8,64,1,4,128]{4,3,1,2,0:T(4,128)(2,1)} %bitcast.10), calls=%async_computation | async-start | bytes 1048576 | tf_op jit(solution)/shard_map/all_to_all | solution.py:119
  17.4 0.4 copy.139
  17.8 14.8 %all-to-all-done = bf16[8,64,1,4,128]{4,3,1,2,0:T(4,128)(2,1)S(1)} async-done(((bf16[8,64,1,4,128]{4,3,1,2,0:T(4,128)(2,1)}), bf16[8,64,1,4,128]{4,3,1,2,0:T(4,128)(2,1)S(1)}, u32[]{:S(2)}, u32[]{:S(2)}) %all-to-all-start) | async-done | bytes 524320 | tf_op jit(solution)/shard_map/all_to_all | solution.py:119
  32.6 1.6 broadcast_in_dim.13
  34.3 4.3 all-to-all-start.2
  38.5 2.5 copy.181
  41.0 2.0 reshape.239
  43.0 32.5 %all-to-all-done.2 = bf16[8,64,1,16,128]{4,3,1,2,0:T(8,128)(2,1)S(1)} async-done(((bf16[8,64,1,16,128]{4,3,1,2,0:T(8,128)(2,1)}), bf16[8,64,1,16,128]{4,3,1,2,0:T(8,128)(2,1)S(1)}, u32[]{:S(2)}, u32[]{:S(2)}) %all-to-all-start.2) | async-done | bytes 2097184 | tf_op jit(solution)/shard_map/all_to_all | solution.py:126
  75.5 24.2 %all-to-all-start.1 = ((bf16[1,64,1,4,1024]{4,3,2,0,1:T(4,128)(2,1)}), bf16[1,64,1,4,1024]{4,3,2,0,1:T(4,128)(2,1)}, u32[]{:S(2)}, u32[]{:S(2)}) async-start(bf16[1,64,1,4,1024]{4,3,2,0,1:T(4,128)(2,1)} %reshape.239), calls=%async_computation.1 | async-start | bytes 1048576 | tf_op jit(solution)/shard_map/all_to_all | solution.py:118
  99.7 1.7 bitcast_bitcast_fusion.1
  101.4 13.1 %all-to-all-done.1 = bf16[1,64,1,4,1024]{4,3,2,0,1:T(4,128)(2,1)} async-done(((bf16[1,64,1,4,1024]{4,3,2,0,1:T(4,128)(2,1)}), bf16[1,64,1,4,1024]{4,3,2,0,1:T(4,128)(2,1)}, u32[]{:S(2)}, u32[]{:S(2)}) %all-to-all-start.1) | async-done | bytes 524320 | tf_op jit(solution)/shard_map/all_to_all | solution.py:118
  114.5 56.3 %all_to_all.150 = bf16[1,64,1,16,1024]{4,3,2,0,1:T(8,128)(2,1)S(1)} all-to-all(bf16[1,64,1,16,1024]{4,3,2,0,1:T(8,128)(2,1)} %bitcast_bitcast_fusion.1), channel_id=1, replica_groups=mesh['row'=64,'ch'=8] {'row'}, dimensions={1} | all-to-all | bytes 4194304 | tf_op jit(solution)/shard_map/all_to_all | solution.py:125
  170.8 1.8 fusion.12
  172.6 0.3 copy.142
  173.0 24.6 %all_to_all.151 = bf16[1,64,4,8,128]{4,3,2,0,1:T(8,128)(2,1)S(1)} all-to-all(bf16[1,64,4,8,128]{4,3,2,0,1:T(8,128)(2,1)S(1)} %copy.142), channel_id=1, replica_groups=mesh['row'=64,'ch'=8] {'row'}, dimensions={1} | all-to-all | bytes 1048576 | tf_op jit(solution)/shard_map/all_to_all | solution.py:145
  197.6 1.0 copy.143
  198.6 9.6 %all-to-all-start.5 = ((bf16[64,1,4,8,128]{4,0,2,1,3:T(8,128)(2,1)}), bf16[64,1,4,8,128]{4,0,2,1,3:T(8,128)(2,1)S(1)}, u32[]{:S(2)}, u32[]{:S(2)}) async-start(bf16[64,1,4,8,128]{4,0,2,1,3:T(8,128)(2,1)} %copy.143), calls=%async_computation.5 | async-start | bytes 1048576 | tf_op jit(solution)/shard_map/all_to_all | solution.py:144
  208.2 0.3 copy.151
  209.1 2.0 fusion.11
  211.1 11.0 %all-to-all-done.5 = bf16[64,1,4,8,128]{4,0,2,1,3:T(8,128)(2,1)S(1)} async-done(((bf16[64,1,4,8,128]{4,0,2,1,3:T(8,128)(2,1)}), bf16[64,1,4,8,128]{4,0,2,1,3:T(8,128)(2,1)S(1)}, u32[]{:S(2)}, u32[]{:S(2)}) %all-to-all-start.5) | async-done | bytes 524320 | tf_op jit(solution)/shard_map/all_to_all | solution.py:144
  222.0 0.4 copy.212
  223.1 1.3 fusion.41
  224.4 0.4 fusion.60
  225.0 0.8 add_bitcast_fusion
  225.8 0.6 fusion.19
  226.4 4.0 reshape.219
  230.5 10.8 %copy.155 = bf16[8,16,1,16,8,4,4]{3,0,6,4,5,1,2:T(8,128)(2,1)} copy(bf16[8,16,1,16,8,4,4]{1,0,6,5,4,3,2:T(8,128)(2,1)} %reshape.219) | data formatting | bytes 1048576 | tf_op jit(solution)/shard_map/reshape | solution.py:107
  241.3 6.5 %copy.156 = bf16[8,64,1,16,32]{1,4,3,2,0:T(8,128)(2,1)S(1)} copy(bf16[8,64,1,16,32]{3,0,4,1,2:T(8,128)(2,1)} %bitcast.173) | data formatting | bytes 1048576 | tf_op jit(solution)/shard_map/reshape | solution.py:110
  247.8 1.5 reshape.262
  249.3 7.6 %all-to-all-start.6 = ((bf16[8,2,16384]{2,1,0:T(2,128)(2,1)}), bf16[8,2,16384]{2,1,0:T(2,128)(2,1)S(1)}, u32[]{:S(2)}, u32[]{:S(2)}) async-start(bf16[8,2,16384]{2,1,0:T(2,128)(2,1)} %reshape.262), calls=%async_computation.6 | async-start | bytes 1048576 | tf_op jit(solution)/shard_map/all_to_all | solution.py:119
  256.9 0.4 copy.160
  257.3 13.8 %all-to-all-done.6 = bf16[8,2,16384]{2,1,0:T(2,128)(2,1)S(1)} async-done(((bf16[8,2,16384]{2,1,0:T(2,128)(2,1)}), bf16[8,2,16384]{2,1,0:T(2,128)(2,1)S(1)}, u32[]{:S(2)}, u32[]{:S(2)}) %all-to-all-start.6) | async-done | bytes 524320 | tf_op jit(solution)/shard_map/all_to_all | solution.py:119
  271.1 1.6 broadcast_in_dim.16
  272.8 7.2 %all-to-all-start.8 = ((bf16[8,64,1,16,128]{4,3,1,2,0:T(8,128)(2,1)}), bf16[8,64,1,16,128]{4,3,1,2,0:T(8,128)(2,1)S(1)}, u32[]{:S(2)}, u32[]{:S(2)}) async-start(bf16[8,64,1,16,128]{4,3,1,2,0:T(8,128)(2,1)} %bitcast.56), calls=%async_computation.8 | async-start | bytes 4194304 | tf_op jit(solution)/shard_map/all_to_all | solution.py:126
  280.0 3.0 reshape.263
  283.0 1.3 bitcast_bitcast_fusion.2
  284.4 1.1 copy.157
  285.4 2.7 copy.158
  288.2 35.8 %all-to-all-done.8 = bf16[8,64,1,16,128]{4,3,1,2,0:T(8,128)(2,1)S(1)} async-done(((bf16[8,64,1,16,128]{4,3,1,2,0:T(8,128)(2,1)}), bf16[8,64,1,16,128]{4,3,1,2,0:T(8,128)(2,1)S(1)}, u32[]{:S(2)}, u32[]{:S(2)}) %all-to-all-start.8) | async-done | bytes 2097184 | tf_op jit(solution)/shard_map/all_to_all | solution.py:126
  324.0 11.2 %all-to-all-start.7 = ((bf16[1,64,1,16,256]{4,3,2,0,1:T(8,128)(2,1)}), bf16[1,64,1,16,256]{4,3,2,0,1:T(8,128)(2,1)}, u32[]{:S(2)}, u32[]{:S(2)}) async-start(bf16[1,64,1,16,256]{4,3,2,0,1:T(8,128)(2,1)} %copy.158), calls=%async_computation.7 | async-start | bytes 1048576 | tf_op jit(solution)/shard_map/all_to_all | solution.py:118
  335.2 1.7 bitcast_bitcast_fusion
  336.9 15.1 %all-to-all-done.7 = bf16[1,64,1,16,256]{4,3,2,0,1:T(8,128)(2,1)} async-done(((bf16[1,64,1,16,256]{4,3,2,0,1:T(8,128)(2,1)}), bf16[1,64,1,16,256]{4,3,2,0,1:T(8,128)(2,1)}, u32[]{:S(2)}, u32[]{:S(2)}) %all-to-all-start.7) | async-done | bytes 524320 | tf_op jit(solution)/shard_map/all_to_all | solution.py:118
  352.0 6.2 %all-to-all-start.9 = ((bf16[1,64,1,16,1024]{4,3,2,0,1:T(8,128)(2,1)}), bf16[1,64,1,16,1024]{4,3,2,0,1:T(8,128)(2,1)S(1)}, u32[]{:S(2)}, u32[]{:S(2)}) async-start(bf16[1,64,1,16,1024]{4,3,2,0,1:T(8,128)(2,1)} %bitcast_bitcast_fusion), calls=%async_computation.9 | async-start | bytes 4194304 | tf_op jit(solution)/shard_map/all_to_all | solution.py:125
  358.2 2.0 copy.159
  360.2 2.0 dot_general.45
  362.2 46.4 %all-to-all-done.9 = bf16[1,64,1,16,1024]{4,3,2,0,1:T(8,128)(2,1)S(1)} async-done(((bf16[1,64,1,16,1024]{4,3,2,0,1:T(8,128)(2,1)}), bf16[1,64,1,16,1024]{4,3,2,0,1:T(8,128)(2,1)S(1)}, u32[]{:S(2)}, u32[]{:S(2)}) %all-to-all-start.9) | async-done | bytes 2097184 | tf_op jit(solution)/shard_map/all_to_all | solution.py:125
  408.7 2.6 copy.163
  411.2 2.5 fusion.13
  413.8 0.3 copy.165
  414.1 24.0 %all_to_all.152 = bf16[1,64,4,8,128]{4,3,2,0,1:T(8,128)(2,1)S(1)} all-to-all(bf16[1,64,4,8,128]{4,3,2,0,1:T(8,128)(2,1)S(1)} %copy.165), channel_id=1, replica_groups=mesh['row'=64,'ch'=8] {'row'}, dimensions={1} | all-to-all | bytes 1048576 | tf_op jit(solution)/shard_map/all_to_all | solution.py:145
  438.1 1.0 copy.166
  439.1 5.8 %all-to-all-start.11 = ((bf16[64,1,4,8,128]{4,0,2,1,3:T(8,128)(2,1)}), bf16[64,1,4,8,128]{4,0,2,1,3:T(8,128)(2,1)S(1)}, u32[]{:S(2)}, u32[]{:S(2)}) async-start(bf16[64,1,4,8,128]{4,0,2,1,3:T(8,128)(2,1)} %copy.166), calls=%async_computation.11 | async-start | bytes 1048576 | tf_op jit(solution)/shard_map/all_to_all | solution.py:144
  445.4 1.5 fusion.7
  446.9 11.9 %all-to-all-done.11 = bf16[64,1,4,8,128]{4,0,2,1,3:T(8,128)(2,1)S(1)} async-done(((bf16[64,1,4,8,128]{4,0,2,1,3:T(8,128)(2,1)}), bf16[64,1,4,8,128]{4,0,2,1,3:T(8,128)(2,1)S(1)}, u32[]{:S(2)}, u32[]{:S(2)}) %all-to-all-start.11) | async-done | bytes 524320 | tf_op jit(solution)/shard_map/all_to_all | solution.py:144
  458.8 0.4 copy.211
  459.8 1.3 fusion.37
  461.2 0.5 fusion.3
  461.6 1.3 copy.174
  (75 shorter events, 2.5 us)
Async XLA Ops:
  0.0 4.6 copy-start
  0.0 4.4 copy-start.8
  0.0 4.5 copy-start.7
  0.0 4.6 copy-start.11
  0.0 4.5 copy-start.10
  0.0 4.6 copy-start.5
  7.2 25.5 %all-to-all-start = ((bf16[8,64,1,4,128]{4,3,1,2,0:T(4,128)(2,1)}), bf16[8,64,1,4,128]{4,3,1,2,0:T(4,128)(2,1)S(1)}, u32[]{:S(2)}, u32[]{:S(2)}) async-start(bf16[8,64,1,4,128]{4,3,1,2,0:T(4,128)(2,1)} %bitcast.10), calls=%async_computation | async-start | bytes 1048576 | tf_op jit(solution)/shard_map/all_to_all | solution.py:119
  32.6 1.6 copy-start.2
  34.3 41.2 %all-to-all-start.2 = ((bf16[8,64,1,16,128]{4,3,1,2,0:T(8,128)(2,1)}), bf16[8,64,1,16,128]{4,3,1,2,0:T(8,128)(2,1)S(1)}, u32[]{:S(2)}, u32[]{:S(2)}) async-start(bf16[8,64,1,16,128]{4,3,1,2,0:T(8,128)(2,1)} %bitcast.17), calls=%async_computation.2 | async-start | bytes 4194304 | tf_op jit(solution)/shard_map/all_to_all | solution.py:126
  75.5 39.0 %all-to-all-start.1 = ((bf16[1,64,1,4,1024]{4,3,2,0,1:T(4,128)(2,1)}), bf16[1,64,1,4,1024]{4,3,2,0,1:T(4,128)(2,1)}, u32[]{:S(2)}, u32[]{:S(2)}) async-start(bf16[1,64,1,4,1024]{4,3,2,0,1:T(4,128)(2,1)} %reshape.239), calls=%async_computation.1 | async-start | bytes 1048576 | tf_op jit(solution)/shard_map/all_to_all | solution.py:118
  197.6 10.9 %copy-start.12 = (f32[2,128]{1,0:T(2,128)S(1)}, f32[2,128]{1,0:T(2,128)}, u32[]{:S(2)}) copy-start(f32[2,128]{1,0:T(2,128)} %param.21) | copy-start | bytes 3076
  197.6 10.9 %copy-start.13 = (f32[2,128]{1,0:T(2,128)S(1)}, f32[2,128]{1,0:T(2,128)}, u32[]{:S(2)}) copy-start(f32[2,128]{1,0:T(2,128)} %param.20) | copy-start | bytes 3076
  197.6 11.4 %copy-start.9 = (f32[2,128]{1,0:T(2,128)S(1)}, f32[2,128]{1,0:T(2,128)}, u32[]{:S(2)}) copy-start(f32[2,128]{1,0:T(2,128)} %param.23) | copy-start | bytes 3076
  197.6 11.5 %copy-start.14 = (bf16[2,128,128]{2,1,0:T(8,128)(2,1)S(1)}, bf16[2,128,128]{2,1,0:T(8,128)(2,1)}, u32[]{:S(2)}) copy-start(bf16[2,128,128]{2,1,0:T(8,128)(2,1)} %param.18) | copy-start | bytes 196612
  198.6 23.4 %all-to-all-start.5 = ((bf16[64,1,4,8,128]{4,0,2,1,3:T(8,128)(2,1)}), bf16[64,1,4,8,128]{4,0,2,1,3:T(8,128)(2,1)S(1)}, u32[]{:S(2)}, u32[]{:S(2)}) async-start(bf16[64,1,4,8,128]{4,0,2,1,3:T(8,128)(2,1)} %copy.143), calls=%async_computation.5 | async-start | bytes 1048576 | tf_op jit(solution)/shard_map/all_to_all | solution.py:144
  223.1 1.3 copy-start.3
  223.1 1.3 copy-start.6
  249.3 21.8 %all-to-all-start.6 = ((bf16[8,2,16384]{2,1,0:T(2,128)(2,1)}), bf16[8,2,16384]{2,1,0:T(2,128)(2,1)S(1)}, u32[]{:S(2)}, u32[]{:S(2)}) async-start(bf16[8,2,16384]{2,1,0:T(2,128)(2,1)} %reshape.262), calls=%async_computation.6 | async-start | bytes 1048576 | tf_op jit(solution)/shard_map/all_to_all | solution.py:119
  271.1 1.6 copy-start.1
  272.8 51.2 %all-to-all-start.8 = ((bf16[8,64,1,16,128]{4,3,1,2,0:T(8,128)(2,1)}), bf16[8,64,1,16,128]{4,3,1,2,0:T(8,128)(2,1)S(1)}, u32[]{:S(2)}, u32[]{:S(2)}) async-start(bf16[8,64,1,16,128]{4,3,1,2,0:T(8,128)(2,1)} %bitcast.56), calls=%async_computation.8 | async-start | bytes 4194304 | tf_op jit(solution)/shard_map/all_to_all | solution.py:126
  324.0 28.0 %all-to-all-start.7 = ((bf16[1,64,1,16,256]{4,3,2,0,1:T(8,128)(2,1)}), bf16[1,64,1,16,256]{4,3,2,0,1:T(8,128)(2,1)}, u32[]{:S(2)}, u32[]{:S(2)}) async-start(bf16[1,64,1,16,256]{4,3,2,0,1:T(8,128)(2,1)} %copy.158), calls=%async_computation.7 | async-start | bytes 1048576 | tf_op jit(solution)/shard_map/all_to_all | solution.py:118
  352.0 56.7 %all-to-all-start.9 = ((bf16[1,64,1,16,1024]{4,3,2,0,1:T(8,128)(2,1)}), bf16[1,64,1,16,1024]{4,3,2,0,1:T(8,128)(2,1)S(1)}, u32[]{:S(2)}, u32[]{:S(2)}) async-start(bf16[1,64,1,16,1024]{4,3,2,0,1:T(8,128)(2,1)} %bitcast_bitcast_fusion), calls=%async_computation.9 | async-start | bytes 4194304 | tf_op jit(solution)/shard_map/all_to_all | solution.py:125
  413.8 31.6 %copy-start.15 = (bf16[2,128,128]{2,1,0:T(8,128)(2,1)S(1)}, bf16[2,128,128]{2,1,0:T(8,128)(2,1)}, u32[]{:S(2)}) copy-start(bf16[2,128,128]{2,1,0:T(8,128)(2,1)} %param.18) | copy-start | bytes 196612
  439.1 19.7 %all-to-all-start.11 = ((bf16[64,1,4,8,128]{4,0,2,1,3:T(8,128)(2,1)}), bf16[64,1,4,8,128]{4,0,2,1,3:T(8,128)(2,1)S(1)}, u32[]{:S(2)}, u32[]{:S(2)}) async-start(bf16[64,1,4,8,128]{4,0,2,1,3:T(8,128)(2,1)} %copy.166), calls=%async_computation.11 | async-start | bytes 1048576 | tf_op jit(solution)/shard_map/all_to_all | solution.py:144
  459.8 1.4 copy-start.4
where the time goes:
time: 467 us; the launch traced here: 463 us
  waiting for transfers between devices  194 us (42%)
  blocking collectives  105 us (22%)
  starting transfers between devices  86.4 us (19%)
  local copies, waits for them, and re-layouts  57.3 us (12%)
  matrix products  10.4 us (2%)
  other arithmetic  9.09 us (2%)
    all_to_all x2, waiting for transfers between devices, local(): lax.all_to_all(send_right, 'ch', split_axis=0, concat_axis=4, tiled=True)  68.3 us
    all_to_all x1, blocking collectives, local(): lax.all_to_all(lax.all_to_all(send_right, 'ch', split_axis=0, concat_axis...  56.3 us
    all_to_all x2, blocking collectives, local(): lax.all_to_all(returned.astype(jnp.bfloat16), 'row', split_axis=1, concat...  48.6 us
    all_to_all x1, waiting for transfers between devices, local(): lax.all_to_all(lax.all_to_all(send_right, 'ch', split_axis=0, concat_axis...  46.4 us
    all_to_all x2, starting transfers between devices, local(): lax.all_to_all(lax.all_to_all(send_left, 'ch', split_axis=0, concat_axis=...  35.5 us
    all_to_all x2, waiting for transfers between devices, local(): lax.all_to_all(send_left, 'ch', split_axis=0, concat_axis=4, tiled=True)  28.6 us
    all_to_all x2, waiting for transfers between devices, local(): lax.all_to_all(lax.all_to_all(send_left, 'ch', split_axis=0, concat_axis=...  28.1 us
    all_to_all x2, waiting for transfers between devices, local(): lax.all_to_all(lax.all_to_all(returned.astype(jnp.bfloat16), 'row', split...  22.8 us
  transfers between devices with their start and end apart: 9, of which 9 were waited for; matrix products, arithmetic and copies ran while one was open for 6% of the time, Pallas kernels for 0%

commit v1 on v0

v1 whole, which is shorter than its diff:
```python
import functools

import jax
import jax.numpy as jnp
from jax import lax
from jax.experimental import pallas as pl
from jax.experimental.pallas import tpu as pltpu
from jax.sharding import PartitionSpec as P

PAIR_EPSILON = 1e-05
HIDDEN_EPSILON = 1.0
MESH = pl.DeviceIdType.MESH
HIDDEN = 128
TILE = 16
LANE = 128


def layer_norm(values, gain_value, shift_value, along, epsilon):
    center = jnp.mean(values, axis=along, keepdims=True)
    offset = values - center
    spread = jnp.mean(offset * offset, axis=along, keepdims=True)
    return offset * lax.rsqrt(spread + epsilon) * gain_value + shift_value


def shuffled(t):
    dz = (5 * t) % 8
    dy = (t // 8 + 3 * t) % 8
    return dz, dy, t // 64


def triangle_kernel(section, left_ref, right_ref, out_ref, abuf, bbuf, xbuf, xrecv, send_sem, recv_sem):
    row = lax.axis_index("row")
    ch = lax.axis_index("ch")
    z, y_lo, x = row // 8, (row // 4) % 2, row % 4
    y_hi, core = ch // 2, ch % 2
    y = y_hi * 2 + y_lo
    x_hi, x_lo = x // 2, x % 2
    hx = x + x_hi * (3 - 2 * x)
    half = x_hi
    own_h = z * 16 + y * 2 + hx

    if section == 0:
        a_half, a_core = x_hi, core
        b_half, b_core = x_hi, z % 2
        a_slot = abuf.at[
            core, pl.ds((z * 4 + y_lo * 2 + x_lo) * TILE, TILE), pl.ds(y_hi * LANE, LANE)
        ]
        b_slot = bbuf.at[
            core, z // 2, y_lo, x_hi, pl.ds(x_lo * TILE, TILE), pl.ds(y_hi * LANE, LANE)
        ]
        a_self = None
        b_self = core == z % 2
    else:
        a_half, a_core = y_hi // 2, core
        b_half, b_core = x_hi, core
        a_slot = abuf.at[core, pl.ds(row * TILE, TILE), pl.ds((y_hi % 2) * LANE, LANE)]
        b_slot = bbuf.at[
            z // 4, z % 4, y_lo, x_hi, pl.ds(x_lo * TILE, TILE), pl.ds(y_hi * LANE, LANE)
        ]
        a_self = y_hi // 2 == x_hi
        b_self = None

    def target(t, to_half, to_core):
        dz, dy, dx = shuffled(t)
        z_t, y_t, hx_t = (z + dz) % 8, (y + dy) % 8, (hx + dx) % 2
        x_t = hx_t + to_half * (3 - 2 * hx_t)
        there = {"row": z_t * 8 + (y_t % 2) * 4 + x_t, "ch": (y_t // 2) * 2 + to_core}
        return z_t * 16 + y_t * 2 + hx_t, there

    def remote(src, dst, sent, got, there):
        return pltpu.make_async_remote_copy(
            src_ref=src,
            dst_ref=dst,
            send_sem=send_sem.at[sent],
            recv_sem=recv_sem.at[got],
            device_id=there,
            device_id_type=MESH,
        )

    def first(src, dst, sent, got, there, to_self):
        local = pltpu.make_async_copy(src, dst, recv_sem.at[got])
        if to_self is None:
            local.start()
        else:
            pl.when(to_self)(local.start)
            pl.when(jnp.logical_not(to_self))(remote(src, dst, sent, got, there).start)

    def first_done(src, sent, to_self):
        if to_self is not None:
            pl.when(jnp.logical_not(to_self))(
                pltpu.make_async_copy(src, src, send_sem.at[sent]).wait
            )

    def panel_sends(ref, slot, to_half, to_core, sent, got, to_self):
        h_0, there_0 = target(0, to_half, to_core)
        first(ref.at[h_0], slot, sent + 1, got, there_0, to_self)

        def body(t, carry):
            h_t, there = target(t, to_half, to_core)
            remote(ref.at[h_t], slot, sent, got, there).start()
            return carry

        lax.fori_loop(1, HIDDEN, body, 0)

    def got_all(got):
        pltpu.make_async_copy(left_ref, left_ref, recv_sem.at[got]).wait()

    def sent_all(sent, to_self):
        rest = left_ref.at[pl.ds(0, HIDDEN - 1)]
        pltpu.make_async_copy(rest, rest, send_sem.at[sent]).wait()
        first_done(left_ref.at[0], sent + 1, to_self)

    panel_sends(right_ref, b_slot, b_half, b_core, 0, 0, b_self)
    panel_sends(left_ref, a_slot, a_half, a_core, 2, 1, a_self)

    got_all(0)
    partner = {"row": row + 3 - 2 * x, "ch": ch}
    for outer in range(2):
        for inner in range(4):
            for low in range(2):
                block = bbuf.at[outer, inner, low, half] if section == 0 else bbuf.at[outer, inner, low, half]
                remote(block, block, 4, 2, partner).start()
    got_all(1)
    sibling = {"row": row, "ch": ch + 1 - 2 * core}
    remote(abuf.at[core], abuf.at[core], 5, 3, sibling).start()
    got_all(2)
    got_all(3)

    if section == 0:
        products = None
        for part in range(2):
            right = bbuf[part].reshape(512, 512)
            term = lax.dot_general(
                abuf[part], right, (((1,), (1,)), ((), ())), preferred_element_type=jnp.float32
            )
            products = term if products is None else products + term
        xbuf[...] = products.astype(jnp.bfloat16)
    else:
        right = bbuf[...].reshape(1024, 512)
        for part in range(2):
            term = lax.dot_general(
                abuf[part], right, (((0,), (0,)), ((), ())), preferred_element_type=jnp.float32
            )
            xbuf[pl.ds(part * 256, 256), :] = term.astype(jnp.bfloat16)

    def cell(t):
        dz, dy, dx = shuffled(t)
        y_t = (y + dy) % 8
        if section == 0:
            z_t, low_t = (z + dz) % 8, (x_lo + dx) % 2
            block = z_t * 4 + (y_t % 2) * 2 + low_t
            row_t = z_t * 8 + (y_t % 2) * 4 + half * 2 + low_t
        else:
            q_t = (z + dz % 4) % 4
            x_t = (x + (dz // 4) * 2 + dx) % 4
            block = (q_t % 2) * 16 + (q_t // 2) * 8 + (y_t % 2) * 4 + x_t
            row_t = half * 32 + q_t * 8 + (y_t % 2) * 4 + x_t
        src = xbuf.at[pl.ds(block * TILE, TILE), pl.ds((y_t // 2) * LANE, LANE)]
        return src, {"row": row_t, "ch": (y_t // 2) * 2 + core}

    x_self = None if section == 0 else z // 4 == half
    src_0, there_0 = cell(0)
    first(src_0, xrecv.at[own_h], 7, 4, there_0, x_self)

    def body(t, carry):
        src, there = cell(t)
        remote(src, xrecv.at[own_h], 6, 4, there).start()
        return carry

    lax.fori_loop(1, HIDDEN, body, 0)
    sent_all(0, b_self)
    sent_all(2, a_self)
    pltpu.make_async_copy(left_ref, left_ref, send_sem.at[4]).wait()
    pltpu.make_async_copy(left_ref, left_ref, send_sem.at[5]).wait()
    got_all(4)
    out_ref[...] = xrecv[...]
    sent_all(6, x_self)


def triangle(section, left_panel, right_panel):
    abuf = (2, 512, 512) if section == 0 else (2, 1024, 256)
    return pl.pallas_call(
        functools.partial(triangle_kernel, section),
        out_shape=jax.ShapeDtypeStruct((HIDDEN, TILE, LANE), jnp.bfloat16),
        in_specs=[pl.BlockSpec(memory_space=pltpu.VMEM)] * 2,
        out_specs=pl.BlockSpec(memory_space=pltpu.VMEM),
        scratch_shapes=[
            pltpu.VMEM(abuf, jnp.bfloat16),
            pltpu.VMEM((2, 4, 2, 2, 32, 512), jnp.bfloat16),
            pltpu.VMEM((512, 512), jnp.bfloat16),
            pltpu.VMEM((HIDDEN, TILE, LANE), jnp.bfloat16),
            pltpu.SemaphoreType.DMA((8,)),
            pltpu.SemaphoreType.DMA((5,)),
        ],
        compiler_params=pltpu.CompilerParams(has_side_effects=True),
        name=f"triangle_{section}",
    )(left_panel, right_panel)


def project(
    current,
    cell_mask,
    section_index,
    pair_gain,
    pair_shift,
    panel_weight,
    panel_bias,
    gate_weight,
    gate_bias,
):
    normed = layer_norm(
        current, pair_gain[section_index], pair_shift[section_index], 2, PAIR_EPSILON
    ).astype(jnp.bfloat16)
    features = jnp.einsum(
        "rjc,cf->frj", normed, panel_weight[section_index], preferred_element_type=jnp.float32
    )
    features = features + panel_bias[section_index][:, None, None]
    left_panel = (
        cell_mask * jax.nn.sigmoid(features[:HIDDEN]) * features[HIDDEN : 2 * HIDDEN]
    ).astype(jnp.bfloat16)
    right_panel = (
        cell_mask
        * jax.nn.sigmoid(features[2 * HIDDEN : 3 * HIDDEN])
        * features[3 * HIDDEN :]
    ).astype(jnp.bfloat16)
    gate_value = jax.nn.sigmoid(
        jnp.einsum(
            "rjc,cd->rjd", normed, gate_weight[section_index], preferred_element_type=jnp.float32
        )
        + gate_bias[section_index]
    )
    return (left_panel, right_panel, gate_value)


def local(
    pair_rep,
    residue_mask,
    pair_gain,
    pair_shift,
    panel_weight,
    panel_bias,
    gate_weight,
    gate_bias,
    hidden_gain,
    hidden_shift,
    output_weight,
    output_bias,
):
    row_count = pair_rep.shape[0]
    col_count = pair_rep.shape[1]
    row_index = lax.axis_index("row")
    col_index = lax.axis_index("ch")
    residue_float = residue_mask.astype(jnp.float32)
    row_mask = lax.dynamic_slice_in_dim(residue_float, row_index * row_count, row_count)
    col_mask = lax.dynamic_slice_in_dim(residue_float, col_index * col_count, col_count)
    cell_mask = row_mask[:, None] * col_mask[None, :]
    current = pair_rep
    for section_index in range(2):
        left_panel, right_panel, gate_value = project(
            current,
            cell_mask,
            section_index,
            pair_gain,
            pair_shift,
            panel_weight,
            panel_bias,
            gate_weight,
            gate_bias,
        )
        gathered = triangle(section_index, left_panel, right_panel).astype(jnp.float32)
        normed = layer_norm(
            gathered,
            hidden_gain[section_index][:, None, None],
            hidden_shift[section_index][:, None, None],
            0,
            HIDDEN_EPSILON,
        ).astype(jnp.bfloat16)
        projected = jnp.einsum(
            "hrj,hc->rjc", normed, output_weight[section_index], preferred_element_type=jnp.float32
        )
        current = current + gate_value * (projected + output_bias[section_index])
    return current


def solution(mesh):
    return jax.shard_map(
        local,
        mesh=mesh,
        in_specs=(P("row", "ch", None), P(), P(), P(), P(), P(), P(), P(), P(), P(), P(), P()),
        out_specs=P("row", "ch", None),
        check_vma=False,
    )
```

time: 467 us -> 201 us (0.43)
  waiting for transfers between devices: 194 us -> 0 us
  Pallas kernels: 0 us -> 153 us
  blocking collectives: 105 us -> 0 us
  starting transfers between devices: 86.4 us -> 0 us
  local copies, waits for them, and re-layouts: 57.3 us -> 14.2 us
  other arithmetic: 9.09 us -> 21.2 us
    all_to_all x9 -> x0, waiting for transfers between devices: 194 us -> none  [the longest x2 68.3 us: local(): lax.all_to_all(send_right, 'ch', split_axis=0, concat_axis=4, tiled=True)]
    pallas_call x0 -> x2, Pallas kernels: none -> 153 us  [triangle(): pl.pallas_call(functools.partial(triangle_kernel, section), out_shape=jax...]
    all_to_all x3 -> x0, blocking collectives: 105 us -> none  [the longest x1 56.3 us: local(): lax.all_to_all(lax.all_to_all(send_right, 'ch', split_axis=0, concat_axis...]
    all_to_all x9 -> x0, starting transfers between devices: 86.4 us -> none  [the longest x2 35.5 us: local(): lax.all_to_all(lax.all_to_all(send_left, 'ch', split_axis=0, concat_axis=...]
    reshape x3 -> x0, local copies, waits for them, and re-layouts: 21.4 us -> none  [the longest x2 14.9 us: local(): left_panel.reshape(col_total, slots, per_slot, row_count, blocks, quarter...]
    all_to_all x9 -> x0, local copies, waits for them, and re-layouts: 14.9 us -> none  [the longest x5 9.56 us: local(): lax.all_to_all(send_left, 'ch', split_axis=0, concat_axis=4, tiled=True)]
    add x0 -> x2, other arithmetic: none -> 6.17 us  [project(): features = features + panel_bias[section_index][:, None, None]]
    unnamed x37 -> x17, local copies, waits for them, and re-layouts: 5.77 us -> 0.38 us
  transfers between devices with their start and end apart: 9 -> 0, of which waited for: 9 -> 0; matrix products, arithmetic and copies ran while one was open for 6% -> 0% of each run, Pallas kernels for 0% -> 0%
where the time goes in v1:
time: 201 us; the launch traced here: 200 us
  Pallas kernels  153 us (76%)
  other arithmetic  21.2 us (11%)
  local copies, waits for them, and re-layouts  14.2 us (7%)
  matrix products  11.1 us (6%)
    pallas_call x2, Pallas kernels, triangle(): pl.pallas_call(functools.partial(triangle_kernel, section), out_shape=jax...  153 us
    dot_general x2, local copies, waits for them, and re-layouts, project(): jnp.einsum('rjc,cf->frj', normed, panel_weight[section_index], preferred_...  10.9 us
    dot_general x2, matrix products, project(): jnp.einsum('rjc,cf->frj', normed, panel_weight[section_index], preferred_...  6.68 us
    add x2, other arithmetic, project(): features = features + panel_bias[section_index][:, None, None]  6.17 us
    reduce_sum x4, other arithmetic, layer_norm(): spread = jnp.mean(offset * offset, axis=along, keepdims=True)  4.44 us

profile of v1, /device:TPU:1, one launch (start us, length us, event | category | flops | bytes accessed | tf_op | source)
XLA Modules:
  0.0 199.7 jit_solution(10433569530943693002)
XLA Ops:
  0.0 0.7 convert_element_type.34
  0.7 0.1 dynamic_slice.6
  0.8 0.1 dynamic_slice.7
  0.8 0.1 broadcast_multiply_fusion
  0.9 0.8 slice_bitcast_fusion.3
  1.7 1.6 reduce_sum.72
  3.3 1.9 multiply_reduce_fusion.1
  5.1 0.8 slice_bitcast_fusion.5
  5.9 3.9 %fusion.48 = f32[16,128,512]{2,1,0:T(8,128)} fusion(bf16[2,128,512]{2,1,0:T(8,128)(2,1)} %param.16, f32[16,128,128]{2,1,0:T(8,128)} %param.12, f32[128]{0:T(128)S(1)} %get-tuple-element.25, f32[128]{0:T(128)S(1)} %get-tuple-element.18, f32[16,128]{1,0:T(8,128)S(1)} %add_rsqrt_fusion.3, f32[16,128]{1,0:T(8,128)S(1)} %broadcast_multiply_fusion.4), kind=kOutput, calls=%fused_computation.70 | convolution fusion | flops 269746176 | bytes 5391360 | tf_op jit(solution)/shard_map/rjc,cf->frj/dot_general | solution.py:214
  9.8 0.0 copy-start.3
  9.8 5.4 %copy.14 = f32[16,128,512]{1,0,2:T(8,128)} copy(f32[16,128,512]{2,1,0:T(8,128)} %fusion.48) | data formatting | bytes 8388608 | tf_op jit(solution)/shard_map/rjc,cf->frj/dot_general | solution.py:214
  15.3 0.0 copy-done.3
  15.3 3.1 %add_bitcast_fusion.1 = f32[512,16,128]{2,1,0:T(8,128)S(1)} fusion(f32[16,128,512]{1,0,2:T(8,128)} %copy.14, f32[512]{0:T(512)S(1)} %bitcast.59), kind=kLoop, calls=%fused_computation.1 | loop fusion | flops 1048576 | bytes 8390656 | tf_op jit(solution)/shard_map/add | solution.py:217
  18.4 0.0 copy-start.5
  18.4 0.0 copy-start.6
  18.4 0.0 copy-start
  18.4 0.0 copy-start.7
  18.4 1.5 fusion.34
  19.9 75.0 %triangle_0.1 = bf16[128,16,128]{2,1,0:T(8,128)(2,1)} custom-call(bf16[128,16,128]{2,1,0:T(8,128)(2,1)} %get-tuple-element.8.left_ref, bf16[128,16,128]{2,1,0:T(8,128)(2,1)} %get-tuple-element.7.right_ref), custom_call_target="tpu_custom_call" | custom-call | tf_op jit(solution)/shard_map/triangle_0/pallas_call | solution.py:182
  95.0 0.0 copy-start.4
  95.0 1.2 convert_reduce_fusion.1
  96.2 1.2 fusion.20
  97.4 0.0 copy-done.5
  97.4 0.0 copy-done.6
  97.5 0.0 copy-start.2
  97.5 1.4 fusion.23
  98.9 0.0 copy-done
  98.9 0.0 copy-done.7
  98.9 2.0 %fusion.11 = f32[16,128,128]{1,2,0:T(8,128)} fusion(f32[128]{0:T(128)S(1)} %get-tuple-element.22, bf16[2,128,128]{2,1,0:T(8,128)(2,1)S(1)} %copy-done.7, f32[16,128,128]{2,1,0:T(8,128)S(1)} %copy-done, f32[128]{0:T(128)S(1)} %get-tuple-element.25, f32[128]{0:T(128)S(1)} %get-tuple-element.18, f32[16,128]{1,0:T(8,128)S(1)} %add_rsqrt_fusion.3, ...), kind=kOutput, calls=%fused_computation.17 | convolution fusion | flops 69468160 | bytes 2147840 | tf_op jit(solution)/shard_map/rjc,cd->rjd/dot_general | solution.py:227
  100.9 0.0 copy-done.4
  100.9 0.0 copy-start.1
  100.9 0.3 copy.17
  101.3 0.0 copy-done.2
  101.3 1.6 fusion.61
  102.9 0.1 multiply_reduce_fusion
  103.0 0.0 copy-done.1
  103.0 2.8 %fusion.46 = f32[16,128,512]{2,1,0:T(8,128)} fusion(bf16[2,128,512]{2,1,0:T(8,128)(2,1)S(1)} %copy-done.1, f32[16,128,128]{1,2,0:T(8,128)S(1)} %get-tuple-element.24, f32[128]{0:T(128)S(1)} %get-tuple-element.26, f32[128]{0:T(128)S(1)} %get-tuple-element.17, f32[16,128]{1,0:T(8,128)S(1)} %add_rsqrt_fusion.1, f32[16,128]{1,0:T(8,128)S(1)} %broadcast_multiply_fusion.2), kind=kOutput, calls=%fused_computation.68 | convolution fusion | flops 269746176 | bytes 5391360 | tf_op jit(solution)/shard_map/rjc,cf->frj/dot_general | solution.py:214
  105.8 5.4 %copy.21 = f32[16,128,512]{1,0,2:T(8,128)} copy(f32[16,128,512]{2,1,0:T(8,128)} %fusion.46) | data formatting | bytes 8388608 | tf_op jit(solution)/shard_map/rjc,cf->frj/dot_general | solution.py:214
  111.2 3.1 %add_bitcast_fusion = f32[512,16,128]{2,1,0:T(8,128)S(1)} fusion(f32[16,128,512]{1,0,2:T(8,128)} %copy.21, f32[512]{0:T(512)S(1)} %bitcast.58), kind=kLoop, calls=%fused_computation | loop fusion | flops 1048576 | bytes 8390656 | tf_op jit(solution)/shard_map/add | solution.py:217
  114.3 1.5 fusion.24
  115.8 77.9 %triangle_1.1 = bf16[128,16,128]{2,1,0:T(8,128)(2,1)} custom-call(bf16[128,16,128]{2,1,0:T(8,128)(2,1)} %get-tuple-element.6.left_ref, bf16[128,16,128]{2,1,0:T(8,128)(2,1)} %get-tuple-element.5.right_ref), custom_call_target="tpu_custom_call" | custom-call | tf_op jit(solution)/shard_map/triangle_1/pallas_call | solution.py:182
  193.7 1.2 convert_reduce_fusion
  194.9 1.2 fusion.16
  196.1 1.4 fusion.19
  197.5 0.5 fusion.7
  198.1 0.3 fusion.3
  198.4 1.3 copy.24
  (11 shorter events, 0.1 us)
Async XLA Ops:
  9.8 5.5 %copy-start.3 = (f32[2,512]{1,0:T(2,128)S(1)}, f32[2,512]{1,0:T(2,128)}, u32[]{:S(2)}) copy-start(f32[2,512]{1,0:T(2,128)} %param.17) | copy-start | bytes 12292
  18.4 79.1 %copy-start.5 = (f32[2,128]{1,0:T(2,128)S(1)}, f32[2,128]{1,0:T(2,128)}, u32[]{:S(2)}) copy-start(f32[2,128]{1,0:T(2,128)} %param.21) | copy-start | bytes 3076
  18.4 79.1 %copy-start.6 = (f32[2,128]{1,0:T(2,128)S(1)}, f32[2,128]{1,0:T(2,128)}, u32[]{:S(2)}) copy-start(f32[2,128]{1,0:T(2,128)} %param.20) | copy-start | bytes 3076
  18.4 80.5 %copy-start = (f32[16,128,128]{2,1,0:T(8,128)S(1)}, f32[16,128,128]{2,1,0:T(8,128)}, u32[]{:S(2)}) copy-start(f32[16,128,128]{2,1,0:T(8,128)} %param.12) | copy-start | bytes 3145732
  18.4 80.5 %copy-start.7 = (bf16[2,128,128]{2,1,0:T(8,128)(2,1)S(1)}, bf16[2,128,128]{2,1,0:T(8,128)(2,1)}, u32[]{:S(2)}) copy-start(bf16[2,128,128]{2,1,0:T(8,128)(2,1)} %param.18) | copy-start | bytes 196612
  95.0 5.9 %copy-start.4 = (f32[2,128]{1,0:T(2,128)S(1)}, f32[2,128]{1,0:T(2,128)}, u32[]{:S(2)}) copy-start(f32[2,128]{1,0:T(2,128)} %param.23) | copy-start | bytes 3076
  97.5 3.8 %copy-start.2 = (bf16[2,128,128]{2,1,0:T(8,128)(2,1)S(1)}, bf16[2,128,128]{2,1,0:T(8,128)(2,1)}, u32[]{:S(2)}) copy-start(bf16[2,128,128]{2,1,0:T(8,128)(2,1)} %param.22) | copy-start | bytes 196612
  100.9 2.1 %copy-start.1 = (bf16[2,128,512]{2,1,0:T(8,128)(2,1)S(1)}, bf16[2,128,512]{2,1,0:T(8,128)(2,1)}, u32[]{:S(2)}) copy-start(bf16[2,128,512]{2,1,0:T(8,128)(2,1)} %param.16) | copy-start | bytes 786436

commit v2 on v1

v2 whole, which is shorter than its diff:
```python
import functools

import jax
import jax.numpy as jnp
from jax import lax
from jax.experimental import pallas as pl
from jax.experimental.pallas import tpu as pltpu
from jax.sharding import PartitionSpec as P

PAIR_EPSILON = 1e-05
HIDDEN_EPSILON = 1.0
MESH = pl.DeviceIdType.MESH
HIDDEN = 128
TILE = 16
LANE = 128
DEVICES = 512
CHANNELS = 8


def sigmoid(values):
    return 0.5 * jnp.tanh(0.5 * values) + 0.5


def shuffled(t):
    dz = (5 * t) % 8
    dy = (t // 8 + 3 * t) % 8
    return dz, dy, t // 64


def evoformer_kernel(
    row_mask_ref,
    hidden_gain_ref,
    hidden_shift_ref,
    pair_ref,
    col_mask_ref,
    pair_gain_ref,
    pair_shift_ref,
    panel_weight_ref,
    panel_bias_ref,
    gate_weight_ref,
    gate_bias_ref,
    output_weight_ref,
    output_bias_ref,
    out_ref,
    weight_buf,
    bias_buf,
    normed_buf,
    gate_buf,
    wide_buf,
    left_send,
    right_send,
    abuf_0,
    abuf_1,
    bbuf_0,
    bbuf_1,
    xbuf,
    xrecv,
    send_sem,
    recv_sem,
):
    row = lax.axis_index("row")
    ch = lax.axis_index("ch")
    z, y_lo, x = row // 8, (row // 4) % 2, row % 4
    y_hi, core = ch // 2, ch % 2
    y = y_hi * 2 + y_lo
    x_hi, x_lo = x // 2, x % 2
    hx = x + x_hi * (3 - 2 * x)
    half = x_hi
    own_h = z * 16 + y * 2 + hx

    barrier = pltpu.get_barrier_semaphore()
    me = row * CHANNELS + ch

    def greet(t, carry):
        other = (me + t) % DEVICES
        there = {"row": other // CHANNELS, "ch": other % CHANNELS}
        pl.semaphore_signal(barrier, inc=1, device_id=there, device_id_type=MESH)
        return carry

    lax.fori_loop(1, DEVICES, greet, 0)

    col_mask = col_mask_ref[pl.ds(ch, 1), :].astype(jnp.float32)

    def prepare(section):
        weight = panel_weight_ref[section].astype(jnp.float32)
        weight_buf[section] = weight.T.astype(jnp.bfloat16)
        bias = panel_bias_ref[pl.ds(section, 1), :]
        bias_buf[section] = jnp.broadcast_to(bias, (LANE, 4 * HIDDEN)).T

    def normalize(section, source):
        gain = pair_gain_ref[pl.ds(section, 1), :]
        shift = pair_shift_ref[pl.ds(section, 1), :]

        def body(r, carry):
            values = source[r]
            offset = values - jnp.mean(values, axis=-1, keepdims=True)
            spread = jnp.mean(offset * offset, axis=-1, keepdims=True)
            normed = offset * lax.rsqrt(spread + PAIR_EPSILON) * gain + shift
            normed_buf[r] = normed.astype(jnp.bfloat16)
            return carry

        lax.fori_loop(0, TILE, body, 0, unroll=4)

    def panel(section, base, send_ref):
        def body(r, carry):
            features = lax.dot_general(
                weight_buf[section, pl.ds(base, 2 * HIDDEN)],
                normed_buf[r],
                (((1,), (1,)), ((), ())),
                preferred_element_type=jnp.float32,
            )
            features = features + bias_buf[section, pl.ds(base, 2 * HIDDEN)]
            mask = col_mask * row_mask_ref[row * TILE + r].astype(jnp.float32)
            values = mask * sigmoid(features[:HIDDEN]) * features[HIDDEN:]
            wide_buf[pl.ds(r, HIDDEN, stride=TILE), :] = values
            return carry

        lax.fori_loop(0, TILE, body, 0, unroll=4)

        def pack(i, carry):
            part = wide_buf[pl.ds(i * 16 * TILE, 16 * TILE), :]
            send_ref[pl.ds(i * 16, 16)] = part.reshape(16, TILE, LANE).astype(jnp.bfloat16)
            return carry

        lax.fori_loop(0, 8, pack, 0)

    def gate(section):
        def body(r, carry):
            values = jnp.dot(
                normed_buf[r], gate_weight_ref[section], preferred_element_type=jnp.float32
            )
            gate_buf[r] = sigmoid(values + gate_bias_ref[pl.ds(section, 1), :])
            return carry

        lax.fori_loop(0, TILE, body, 0, unroll=4)

    def finish(section, source):
        got = xrecv.at[section]

        def total(i, carry):
            return carry + jnp.sum(got[pl.ds(i * 16, 16)].astype(jnp.float32), axis=0)

        zero = jnp.zeros((TILE, LANE), jnp.float32)
        center = lax.fori_loop(0, 8, total, zero) * (1.0 / HIDDEN)

        def squares(i, carry):
            offset = got[pl.ds(i * 16, 16)].astype(jnp.float32) - center
            return carry + jnp.sum(offset * offset, axis=0)

        spread = lax.fori_loop(0, 8, squares, zero) * (1.0 / HIDDEN)
        scale = lax.rsqrt(spread + HIDDEN_EPSILON)

        def rescale(h, carry):
            offset = got[h].astype(jnp.float32) - center
            values = offset * scale * hidden_gain_ref[section, h] + hidden_shift_ref[section, h]
            wide_buf[pl.ds(pl.multiple_of(h * TILE, TILE), TILE), :] = values
            return carry

        lax.fori_loop(0, HIDDEN, rescale, 0, unroll=8)

        def body(r, carry):
            normed = wide_buf[pl.ds(r, HIDDEN, stride=TILE), :].astype(jnp.bfloat16)
            projected = lax.dot_general(
                normed,
                output_weight_ref[section],
                (((0,), (0,)), ((), ())),
                preferred_element_type=jnp.float32,
            )
            projected = projected + output_bias_ref[pl.ds(section, 1), :]
            out_ref[r] = source[r] + gate_buf[r] * projected
            return carry

        lax.fori_loop(0, TILE, body, 0, unroll=4)

    def remote(src, dst, sent, got, there):
        return pltpu.make_async_remote_copy(
            src_ref=src,
            dst_ref=dst,
            send_sem=send_sem.at[sent],
            recv_sem=recv_sem.at[got],
            device_id=there,
            device_id_type=MESH,
        )

    def first(src, dst, sent, got, there, to_self):
        local = pltpu.make_async_copy(src, dst, recv_sem.at[got])
        if to_self is None:
            local.start()
        else:
            pl.when(to_self)(local.start)
            pl.when(jnp.logical_not(to_self))(remote(src, dst, sent, got, there).start)

    def got_all(got):
        pltpu.make_async_copy(left_send, left_send, recv_sem.at[got]).wait()

    def sent_all(sent):
        pltpu.make_async_copy(left_send, left_send, send_sem.at[sent]).wait()

    def sent_rest(sent, to_self):
        rest = left_send.at[pl.ds(0, HIDDEN - 1)]
        pltpu.make_async_copy(rest, rest, send_sem.at[sent]).wait()
        if to_self is not None:
            one = left_send.at[0]
            pl.when(jnp.logical_not(to_self))(
                pltpu.make_async_copy(one, one, send_sem.at[sent + 1]).wait
            )

    def target(t, to_half, to_core):
        dz, dy, dx = shuffled(t)
        z_t, y_t, hx_t = (z + dz) % 8, (y + dy) % 8, (hx + dx) % 2
        x_t = hx_t + to_half * (3 - 2 * hx_t)
        there = {"row": z_t * 8 + (y_t % 2) * 4 + x_t, "ch": (y_t // 2) * 2 + to_core}
        return z_t * 16 + y_t * 2 + hx_t, there

    def panel_sends(ref, slot, to_half, to_core, sent, got, to_self):
        h_0, there_0 = target(0, to_half, to_core)
        first(ref.at[h_0], slot, sent + 1, got, there_0, to_self)

        def body(t, carry):
            h_t, there = target(t, to_half, to_core)
            remote(ref.at[h_t], slot, sent, got, there).start()
            return carry

        lax.fori_loop(1, HIDDEN, body, 0)

    partner = {"row": row + 3 - 2 * x, "ch": ch}
    sibling = {"row": row, "ch": ch + 1 - 2 * core}

    def update(section, source):
        abuf = abuf_0 if section == 0 else abuf_1
        bbuf = bbuf_0 if section == 0 else bbuf_1
        sends, gots = 8 * section, 5 * section
        lanes = pl.ds(x_lo * TILE, TILE), pl.ds(y_hi * LANE, LANE)
        if section == 0:
            a_half, a_core = x_hi, core
            b_half, b_core = x_hi, z % 2
            a_slot = abuf.at[core, pl.ds((z * 4 + y_lo * 2 + x_lo) * TILE, TILE), lanes[1]]
            b_slot = bbuf.at[core, z // 2, y_lo, x_hi, lanes[0], lanes[1]]
            a_self, b_self = None, core == z % 2
        else:
            a_half, a_core = y_hi // 2, core
            b_half, b_core = x_hi, core
            a_slot = abuf.at[core, pl.ds(row * TILE, TILE), pl.ds((y_hi % 2) * LANE, LANE)]
            b_slot = bbuf.at[z // 4, z % 4, y_lo, x_hi, lanes[0], lanes[1]]
            a_self, b_self = y_hi // 2 == x_hi, None

        normalize(section, source)
        panel(section, 2 * HIDDEN, right_send)
        if section == 0:
            pl.semaphore_wait(barrier, DEVICES - 1)
        panel_sends(right_send, b_slot, b_half, b_core, sends, gots, b_self)
        panel(section, 0, left_send)
        panel_sends(left_send, a_slot, a_half, a_core, sends + 2, gots + 1, a_self)
        gate(section)

        got_all(gots)
        for outer in range(2):
            for inner in range(4):
                for low in range(2):
                    block = bbuf.at[outer, inner, low, half]
                    remote(block, block, sends + 4, gots + 2, partner).start()
        got_all(gots + 1)
        remote(abuf.at[core], abuf.at[core], sends + 5, gots + 3, sibling).start()
        got_all(gots + 2)
        got_all(gots + 3)

        if section == 0:
            products = None
            for part in range(2):
                term = lax.dot_general(
                    abuf[part],
                    bbuf[part].reshape(512, 512),
                    (((1,), (1,)), ((), ())),
                    preferred_element_type=jnp.float32,
                )
                products = term if products is None else products + term
            xbuf[section] = products.astype(jnp.bfloat16)
        else:
            right = bbuf[...].reshape(1024, 512)
            for part in range(2):
                term = lax.dot_general(
                    abuf[part], right, (((0,), (0,)), ((), ())), preferred_element_type=jnp.float32
                )
                xbuf[section, pl.ds(part * 256, 256), :] = term.astype(jnp.bfloat16)

        def cell(t):
            dz, dy, dx = shuffled(t)
            y_t = (y + dy) % 8
            if section == 0:
                z_t, low_t = (z + dz) % 8, (x_lo + dx) % 2
                block = z_t * 4 + (y_t % 2) * 2 + low_t
                row_t = z_t * 8 + (y_t % 2) * 4 + half * 2 + low_t
            else:
                q_t = (z + dz % 4) % 4
                x_t = (x + (dz // 4) * 2 + dx) % 4
                block = (q_t % 2) * 16 + (q_t // 2) * 8 + (y_t % 2) * 4 + x_t
                row_t = half * 32 + q_t * 8 + (y_t % 2) * 4 + x_t
            src = xbuf.at[section, pl.ds(block * TILE, TILE), pl.ds((y_t // 2) * LANE, LANE)]
            return src, {"row": row_t, "ch": (y_t // 2) * 2 + core}

        x_self = None if section == 0 else z // 4 == half
        x_slot = xrecv.at[section, own_h]
        src_0, there_0 = cell(0)
        first(src_0, x_slot, sends + 7, gots + 4, there_0, x_self)

        def body(t, carry):
            src, there = cell(t)
            remote(src, x_slot, sends + 6, gots + 4, there).start()
            return carry

        lax.fori_loop(1, HIDDEN, body, 0)
        sent_rest(sends, b_self)
        sent_rest(sends + 2, a_self)
        sent_all(sends + 4)
        sent_all(sends + 5)
        got_all(gots + 4)
        finish(section, source)
        sent_rest(sends + 6, x_self)

    prepare(0)
    prepare(1)
    update(0, pair_ref)
    update(1, out_ref)


def local(
    pair_rep,
    residue_mask,
    pair_gain,
    pair_shift,
    panel_weight,
    panel_bias,
    gate_weight,
    gate_bias,
    hidden_gain,
    hidden_shift,
    output_weight,
    output_bias,
):
    smem = pl.BlockSpec(memory_space=pltpu.SMEM)
    vmem = pl.BlockSpec(memory_space=pltpu.VMEM)
    half = jnp.bfloat16
    return pl.pallas_call(
        evoformer_kernel,
        out_shape=jax.ShapeDtypeStruct(pair_rep.shape, jnp.float32),
        in_specs=[smem] * 3 + [vmem] * 10,
        out_specs=vmem,
        scratch_shapes=[
            pltpu.VMEM((2, 4 * HIDDEN, LANE), half),
            pltpu.VMEM((2, 4 * HIDDEN, LANE), jnp.float32),
            pltpu.VMEM((TILE, LANE, LANE), half),
            pltpu.VMEM((TILE, LANE, LANE), jnp.float32),
            pltpu.VMEM((HIDDEN * TILE, LANE), jnp.float32),
            pltpu.VMEM((HIDDEN, TILE, LANE), half),
            pltpu.VMEM((HIDDEN, TILE, LANE), half),
            pltpu.VMEM((2, 512, 512), half),
            pltpu.VMEM((2, 1024, 256), half),
            pltpu.VMEM((2, 4, 2, 2, 32, 512), half),
            pltpu.VMEM((2, 4, 2, 2, 32, 512), half),
            pltpu.VMEM((2, 512, 512), half),
            pltpu.VMEM((2, HIDDEN, TILE, LANE), half),
            pltpu.SemaphoreType.DMA((16,)),
            pltpu.SemaphoreType.DMA((10,)),
        ],
        compiler_params=pltpu.CompilerParams(collective_id=0, has_side_effects=True),
        name="evoformer",
    )(
        residue_mask,
        hidden_gain,
        hidden_shift,
        pair_rep,
        residue_mask.reshape(CHANNELS, LANE),
        pair_gain,
        pair_shift,
        panel_weight,
        panel_bias,
        gate_weight,
        gate_bias,
        output_weight,
        output_bias,
    )


def solution(mesh):
    return jax.shard_map(
        local,
        mesh=mesh,
        in_specs=(P("row", "ch", None), P(), P(), P(), P(), P(), P(), P(), P(), P(), P(), P()),
        out_specs=P("row", "ch", None),
        check_vma=False,
    )
```

time: 201 us -> 146 us (0.73)
  other arithmetic: 21.2 us -> 0 us
  local copies, waits for them, and re-layouts: 14.2 us -> 2.3 us
  matrix products: 11.1 us -> 0 us
  Pallas kernels: 153 us -> 143 us
    dot_general x6 -> x0, matrix products: 11.1 us -> none  [the longest x2 6.68 us: project(): jnp.einsum('rjc,cf->frj', normed, panel_weight[section_index], preferred_...]
    dot_general x2 -> x0, local copies, waits for them, and re-layouts: 10.9 us -> none  [project(): jnp.einsum('rjc,cf->frj', normed, panel_weight[section_index], preferred_...]
    pallas_call x2 -> x1, Pallas kernels: 153 us -> 143 us  [local(): pl.pallas_call(evoformer_kernel, out_shape=jax.ShapeDtypeStruct(pair_rep....]
    reduce_sum x7 -> x0, other arithmetic: 8.37 us -> none  [the longest x4 4.44 us: layer_norm(): spread = jnp.mean(offset * offset, axis=along, keepdims=True)]
    convert_element_type x5 -> x0, other arithmetic: 6.52 us -> none  [the longest x2 3.04 us: project(): right_panel = (cell_mask * jax.nn.sigmoid(features[2 * HIDDEN:3 * HIDDEN]...]
    add x2 -> x0, other arithmetic: 6.17 us -> none  [project(): features = features + panel_bias[section_index][:, None, None]]
    add x4 -> x0, local copies, waits for them, and re-layouts: 2.08 us -> none  [the longest x2 1.31 us: local(): current = current + gate_value * (projected + output_bias[section_index])]
where the time goes in v2:
time: 146 us
  Pallas kernels  143 us (98%)
  local copies, waits for them, and re-layouts  2.3 us (2%)
    pallas_call x1, Pallas kernels, local(): pl.pallas_call(evoformer_kernel, out_shape=jax.ShapeDtypeStruct(pair_rep....  143 us

profile of v2, /device:TPU:1, one launch (start us, length us, event | category | flops | bytes accessed | tf_op | source)
XLA Modules:
  0.0 145.6 jit_solution(12815329634222763527)
XLA Ops:
  0.0 143.3 %evoformer.1 = f32[16,128,128]{2,1,0:T(8,128)} custom-call(s32[1024]{0:T(1024)} %row_mask_ref.1, f32[2,128]{1,0:T(2,128)} %hidden_gain_ref.1, f32[2,128]{1,0:T(2,128)} %hidden_shift_ref.1, f32[16,128,128]{2,1,0:T(8,128)} %pair_ref.1, s32[8,128]{1,0:T(8,128)} %bitcast.1, f32[2,128]{1,0:T(2,128)} %pair_gain_ref.1, f32[2,128]{1,0:T(2,128)} %pair_shift_ref.1, ...), custom_call_target="tpu_custom_call" | custom-call | tf_op jit(solution)/shard_map/evoformer/pallas_call | solution.py:343
  143.3 2.3 %copy.14 = f32[16,128,128]{2,1,0:T(8,128)} copy(f32[16,128,128]{2,1,0:T(8,128)} %evoformer.1) | data formatting | bytes 2097152

commit v3 on v2

--- a/solution.py
+++ b/solution.py
@@ -13,7 +13,6 @@
 HIDDEN = 128
 TILE = 16
 LANE = 128
-DEVICES = 512
 CHANNELS = 8
 
 
@@ -42,6 +41,7 @@
     output_weight_ref,
     output_bias_ref,
     out_ref,
+    pair_buf,
     weight_buf,
     bias_buf,
     normed_buf,
@@ -49,14 +49,14 @@
     wide_buf,
     left_send,
     right_send,
-    abuf_0,
-    abuf_1,
-    bbuf_0,
-    bbuf_1,
+    pair_bufs,
+    core_bufs,
     xbuf,
     xrecv,
     send_sem,
     recv_sem,
+    io_sem,
+    ready_sem,
 ):
     row = lax.axis_index("row")
     ch = lax.axis_index("ch")
@@ -69,15 +69,26 @@
     own_h = z * 16 + y * 2 + hx
 
     barrier = pltpu.get_barrier_semaphore()
-    me = row * CHANNELS + ch
-
-    def greet(t, carry):
-        other = (me + t) % DEVICES
-        there = {"row": other // CHANNELS, "ch": other % CHANNELS}
-        pl.semaphore_signal(barrier, inc=1, device_id=there, device_id_type=MESH)
-        return carry
-
-    lax.fori_loop(1, DEVICES, greet, 0)
+    load = pltpu.make_async_copy(pair_ref, pair_buf, io_sem.at[0])
+    load.start()
+
+    def column(t):
+        spot = (y_lo * CHANNELS + ch + t) % 16
+        return {"row": z * 8 + (spot // CHANNELS) * 4 + x, "ch": spot % CHANNELS}
+
+    def plane(t):
+        spot = (z * 4 + x + t) % 32
+        return {"row": (spot // 4) * 8 + y_lo * 4 + spot % 4, "ch": ch}
+
+    def signals(sem, group, count):
+        def body(t, carry):
+            pl.semaphore_signal(sem, inc=1, device_id=group(t), device_id_type=MESH)
+            return carry
+
+        lax.fori_loop(1, count, body, 0)
+
+    signals(barrier, plane, 32)
+    signals(barrier, column, 16)
 
     col_mask = col_mask_ref[pl.ds(ch, 1), :].astype(jnp.float32)
 
@@ -87,12 +98,12 @@
         bias = panel_bias_ref[pl.ds(section, 1), :]
         bias_buf[section] = jnp.broadcast_to(bias, (LANE, 4 * HIDDEN)).T
 
-    def normalize(section, source):
+    def normalize(section):
         gain = pair_gain_ref[pl.ds(section, 1), :]
         shift = pair_shift_ref[pl.ds(section, 1), :]
 
         def body(r, carry):
-            values = source[r]
+            values = pair_buf[r]
             offset = values - jnp.mean(values, axis=-1, keepdims=True)
             spread = jnp.mean(offset * offset, axis=-1, keepdims=True)
             normed = offset * lax.rsqrt(spread + PAIR_EPSILON) * gain + shift
@@ -134,7 +145,7 @@
 
         lax.fori_loop(0, TILE, body, 0, unroll=4)
 
-    def finish(section, source):
+    def finish(section):
         got = xrecv.at[section]
 
         def total(i, carry):
@@ -167,10 +178,17 @@
                 preferred_element_type=jnp.float32,
             )
             projected = projected + output_bias_ref[pl.ds(section, 1), :]
-            out_ref[r] = source[r] + gate_buf[r] * projected
-            return carry
-
-        lax.fori_loop(0, TILE, body, 0, unroll=4)
+            pair_buf[r] = pair_buf[r] + gate_buf[r] * projected
+            return carry
+
+        for part in range(4):
+            lax.fori_loop(part * 4, part * 4 + 4, body, 0, unroll=4)
+            if section == 1:
+                store(part).start()
+
+    def store(part):
+        some = pl.ds(part * 4, 4)
+        return pltpu.make_async_copy(pair_buf.at[some], out_ref.at[some], io_sem.at[1 + part])
 
     def remote(src, dst, sent, got, there):
         return pltpu.make_async_remote_copy(
@@ -212,76 +230,89 @@
         there = {"row": z_t * 8 + (y_t % 2) * 4 + x_t, "ch": (y_t // 2) * 2 + to_core}
         return z_t * 16 + y_t * 2 + hx_t, there
 
-    def panel_sends(ref, slot, to_half, to_core, sent, got, to_self):
+    def panel_sends(ref, slot, to_half, to_core, sent, gots, to_self):
         h_0, there_0 = target(0, to_half, to_core)
-        first(ref.at[h_0], slot, sent + 1, got, there_0, to_self)
-
-        def body(t, carry):
-            h_t, there = target(t, to_half, to_core)
-            remote(ref.at[h_t], slot, sent, got, there).start()
-            return carry
-
-        lax.fori_loop(1, HIDDEN, body, 0)
+        first(ref.at[h_0], slot, sent + 1, gots[0], there_0, to_self)
+
+        def sends(got):
+            def body(t, carry):
+                h_t, there = target(t, to_half, to_core)
+                remote(ref.at[h_t], slot, sent, got, there).start()
+                return carry
+
+            return body
+
+        lax.fori_loop(1, 64, sends(gots[0]), 0)
+        lax.fori_loop(64, HIDDEN, sends(gots[1]), 0)
 
     partner = {"row": row + 3 - 2 * x, "ch": ch}
     sibling = {"row": row, "ch": ch + 1 - 2 * core}
 
-    def update(section, source):
-        abuf = abuf_0 if section == 0 else abuf_1
-        bbuf = bbuf_0 if section == 0 else bbuf_1
-        sends, gots = 8 * section, 5 * section
-        lanes = pl.ds(x_lo * TILE, TILE), pl.ds(y_hi * LANE, LANE)
+    def update(section):
+        pair_panel = pair_bufs.at[section]
+        core_panel = core_bufs.at[section]
+        s, g = 8 * section, 6 * section
+        rows, lanes = pl.ds(x_lo * TILE, TILE), pl.ds(y_hi * LANE, LANE)
         if section == 0:
-            a_half, a_core = x_hi, core
-            b_half, b_core = x_hi, z % 2
-            a_slot = abuf.at[core, pl.ds((z * 4 + y_lo * 2 + x_lo) * TILE, TILE), lanes[1]]
-            b_slot = bbuf.at[core, z // 2, y_lo, x_hi, lanes[0], lanes[1]]
-            a_self, b_self = None, core == z % 2
+            pair_base, core_base = 2 * HIDDEN, 0
+            pair_slot = pair_panel.at[core, z // 2, y_lo, x_hi, rows, lanes]
+            core_slot = core_panel.at[core, pl.ds((z * 4 + y_lo * 2 + x_lo) * TILE, TILE), lanes]
+            pair_to, core_to = (x_hi, z % 2), (x_hi, core)
+            pair_self, core_self, x_self = core == z % 2, None, None
         else:
-            a_half, a_core = y_hi // 2, core
-            b_half, b_core = x_hi, core
-            a_slot = abuf.at[core, pl.ds(row * TILE, TILE), pl.ds((y_hi % 2) * LANE, LANE)]
-            b_slot = bbuf.at[z // 4, z % 4, y_lo, x_hi, lanes[0], lanes[1]]
-            a_self, b_self = y_hi // 2 == x_hi, None
-
-        normalize(section, source)
-        panel(section, 2 * HIDDEN, right_send)
+            pair_base, core_base = 0, 2 * HIDDEN
+            block = pl.ds(((y_hi % 2) * 2 + core) * LANE, LANE)
+            pair_slot = pair_panel.at[z // 4, z % 4, y_lo, x_hi, rows, block]
+            core_slot = core_panel.at[z // 4, pl.ds((row % 32) * TILE, TILE), lanes]
+            pair_to, core_to = (x_hi, y_hi // 2), (core, z // 4)
+            pair_self = core == y_hi // 2
+            core_self = x_self = jnp.logical_and(core == z // 4, core == x_hi)
+
+        normalize(section)
         if section == 0:
-            pl.semaphore_wait(barrier, DEVICES - 1)
-        panel_sends(right_send, b_slot, b_half, b_core, sends, gots, b_self)
-        panel(section, 0, left_send)
-        panel_sends(left_send, a_slot, a_half, a_core, sends + 2, gots + 1, a_self)
+            pl.semaphore_wait(barrier, 46)
+            signals(ready_sem, plane, 32)
+        panel(section, pair_base, right_send)
+        if section == 0:
+            pl.semaphore_wait(ready_sem, 31)
+        panel_sends(right_send, pair_slot, *pair_to, s, (g, g + 1), pair_self)
+        panel(section, core_base, left_send)
+        panel_sends(left_send, core_slot, *core_to, s + 2, (g + 2, g + 2), core_self)
         gate(section)
 
-        got_all(gots)
-        for outer in range(2):
-            for inner in range(4):
-                for low in range(2):
-                    block = bbuf.at[outer, inner, low, half]
-                    remote(block, block, sends + 4, gots + 2, partner).start()
-        got_all(gots + 1)
-        remote(abuf.at[core], abuf.at[core], sends + 5, gots + 3, sibling).start()
-        got_all(gots + 2)
-        got_all(gots + 3)
+        for dx in range(2):
+            tiles = left_send.at[pl.ds(0, HIDDEN // 2)]
+            pltpu.make_async_copy(tiles, tiles, recv_sem.at[g + dx]).wait()
+            hx_s = (hx + dx) % 2
+            from_rows = pl.ds((hx_s + half * (1 - 2 * hx_s)) * TILE, TILE)
+            for outer in range(2):
+                for inner in range(4):
+                    for low in range(2):
+                        block = pair_panel.at[outer, inner, low, half, from_rows]
+                        remote(block, block, s + 4, g + 3, partner).start()
+        got_all(g + 2)
+        remote(core_panel.at[core], core_panel.at[core], s + 5, g + 4, sibling).start()
+        got_all(g + 3)
+        got_all(g + 4)
 
         if section == 0:
             products = None
             for part in range(2):
                 term = lax.dot_general(
-                    abuf[part],
-                    bbuf[part].reshape(512, 512),
+                    core_bufs[section, part],
+                    pair_bufs[section, part].reshape(512, 512),
                     (((1,), (1,)), ((), ())),
                     preferred_element_type=jnp.float32,
                 )
                 products = term if products is None else products + term
-            xbuf[section] = products.astype(jnp.bfloat16)
         else:
-            right = bbuf[...].reshape(1024, 512)
-            for part in range(2):
-                term = lax.dot_general(
-                    abuf[part], right, (((0,), (0,)), ((), ())), preferred_element_type=jnp.float32
-                )
-                xbuf[section, pl.ds(part * 256, 256), :] = term.astype(jnp.bfloat16)
+            products = lax.dot_general(
+                pair_bufs[section].reshape(1024, 512),
+                core_bufs[section].reshape(1024, 512),
+                (((0,), (0,)), ((), ())),
+                preferred_element_type=jnp.float32,
+            )
+        xbuf[section] = products.astype(jnp.bfloat16)
 
         def cell(t):
             dz, dy, dx = shuffled(t)
@@ -290,37 +321,41 @@
                 z_t, low_t = (z + dz) % 8, (x_lo + dx) % 2
                 block = z_t * 4 + (y_t % 2) * 2 + low_t
                 row_t = z_t * 8 + (y_t % 2) * 4 + half * 2 + low_t
+                core_t = core
             else:
                 q_t = (z + dz % 4) % 4
                 x_t = (x + (dz // 4) * 2 + dx) % 4
-                block = (q_t % 2) * 16 + (q_t // 2) * 8 + (y_t % 2) * 4 + x_t
-                row_t = half * 32 + q_t * 8 + (y_t % 2) * 4 + x_t
+                block = q_t * 8 + (y_t % 2) * 4 + x_t
+                row_t = core * 32 + block
+                core_t = half
             src = xbuf.at[section, pl.ds(block * TILE, TILE), pl.ds((y_t // 2) * LANE, LANE)]
-            return src, {"row": row_t, "ch": (y_t // 2) * 2 + core}
-
-        x_self = None if section == 0 else z // 4 == half
+            return src, {"row": row_t, "ch": (y_t // 2) * 2 + core_t}
+
         x_slot = xrecv.at[section, own_h]
         src_0, there_0 = cell(0)
-        first(src_0, x_slot, sends + 7, gots + 4, there_0, x_self)
+        first(src_0, x_slot, s + 7, g + 5, there_0, x_self)
 
         def body(t, carry):
             src, there = cell(t)
-            remote(src, x_slot, sends + 6, gots + 4, there).start()
+            remote(src, x_slot, s + 6, g + 5, there).start()
             return carry
 
         lax.fori_loop(1, HIDDEN, body, 0)
-        sent_rest(sends, b_self)
-        sent_rest(sends + 2, a_self)
-        sent_all(sends + 4)
-        sent_all(sends + 5)
-        got_all(gots + 4)
-        finish(section, source)
-        sent_rest(sends + 6, x_self)
+        sent_rest(s, pair_self)
+        sent_rest(s + 2, core_self)
+        sent_all(s + 4)
+        sent_all(s + 5)
+        got_all(g + 5)
+        finish(section)
+        sent_rest(s + 6, x_self)
 
     prepare(0)
     prepare(1)
-    update(0, pair_ref)
-    update(1, out_ref)
+    load.wait()
+    update(0)
+    update(1)
+    for part in range(4):
+        store(part).wait()
 
 
 def local(
@@ -343,9 +378,10 @@
     return pl.pallas_call(
         evoformer_kernel,
         out_shape=jax.ShapeDtypeStruct(pair_rep.shape, jnp.float32),
-        in_specs=[smem] * 3 + [vmem] * 10,
-        out_specs=vmem,
+        in_specs=[smem] * 3 + [pl.BlockSpec(memory_space=pl.ANY)] + [vmem] * 9,
+        out_specs=pl.BlockSpec(memory_space=pl.ANY),
         scratch_shapes=[
+            pltpu.VMEM((TILE, LANE, LANE), jnp.float32),
             pltpu.VMEM((2, 4 * HIDDEN, LANE), half),
             pltpu.VMEM((2, 4 * HIDDEN, LANE), jnp.float32),
             pltpu.VMEM((TILE, LANE, LANE), half),
@@ -353,14 +389,14 @@
             pltpu.VMEM((HIDDEN * TILE, LANE), jnp.float32),
             pltpu.VMEM((HIDDEN, TILE, LANE), half),
             pltpu.VMEM((HIDDEN, TILE, LANE), half),
-            pltpu.VMEM((2, 512, 512), half),
-            pltpu.VMEM((2, 1024, 256), half),
-            pltpu.VMEM((2, 4, 2, 2, 32, 512), half),
-            pltpu.VMEM((2, 4, 2, 2, 32, 512), half),
+            pltpu.VMEM((2, 2, 4, 2, 2, 32, 512), half),
+            pltpu.VMEM((2, 2, 512, 512), half),
             pltpu.VMEM((2, 512, 512), half),
             pltpu.VMEM((2, HIDDEN, TILE, LANE), half),
             pltpu.SemaphoreType.DMA((16,)),
-            pltpu.SemaphoreType.DMA((10,)),
+            pltpu.SemaphoreType.DMA((12,)),
+            pltpu.SemaphoreType.DMA((5,)),
+            pltpu.SemaphoreType.REGULAR,
         ],
         compiler_params=pltpu.CompilerParams(collective_id=0, has_side_effects=True),
         name="evoformer",

time: 146 us -> 127 us (0.87)
  Pallas kernels: 143 us -> 125 us
    pallas_call x1, Pallas kernels: 143 us -> 125 us  [local(): pl.pallas_call(evoformer_kernel, out_shape=jax.ShapeDtypeStruct(pair_rep....]
where the time goes in v3:
time: 127 us
  Pallas kernels  125 us (98%)
  local copies, waits for them, and re-layouts  2.3 us (2%)
    pallas_call x1, Pallas kernels, local(): pl.pallas_call(evoformer_kernel, out_shape=jax.ShapeDtypeStruct(pair_rep....  125 us

profile of v3, /device:TPU:1, one launch (start us, length us, event | category | flops | bytes accessed | tf_op | source)
XLA Modules:
  0.0 127.0 jit_solution(17156651066162225500)
XLA Ops:
  0.0 124.7 %evoformer.1 = f32[16,128,128]{2,1,0:T(8,128)} custom-call(s32[1024]{0:T(1024)} %row_mask_ref.1, f32[2,128]{1,0:T(2,128)} %hidden_gain_ref.1, f32[2,128]{1,0:T(2,128)} %hidden_shift_ref.1, f32[16,128,128]{2,1,0:T(8,128)} %pair_ref.1, s32[8,128]{1,0:T(8,128)} %bitcast.1, f32[2,128]{1,0:T(2,128)} %pair_gain_ref.1, f32[2,128]{1,0:T(2,128)} %pair_shift_ref.1, ...), custom_call_target="tpu_custom_call" | custom-call | tf_op jit(solution)/shard_map/evoformer/pallas_call | solution.py:378
  124.7 2.3 %copy.14 = f32[16,128,128]{2,1,0:T(8,128)} copy(f32[16,128,128]{2,1,0:T(8,128)} %evoformer.1) | data formatting | bytes 2097152

commit v4 on v3

--- a/solution.py
+++ b/solution.py
@@ -20,44 +20,59 @@
     return 0.5 * jnp.tanh(0.5 * values) + 0.5
 
 
-def shuffled(t):
-    dz = (5 * t) % 8
-    dy = (t // 8 + 3 * t) % 8
-    return dz, dy, t // 64
-
-
-def evoformer_kernel(
-    row_mask_ref,
-    hidden_gain_ref,
-    hidden_shift_ref,
-    pair_ref,
-    col_mask_ref,
-    pair_gain_ref,
-    pair_shift_ref,
-    panel_weight_ref,
-    panel_bias_ref,
-    gate_weight_ref,
-    gate_bias_ref,
-    output_weight_ref,
-    output_bias_ref,
-    out_ref,
-    pair_buf,
-    weight_buf,
-    bias_buf,
-    normed_buf,
-    gate_buf,
-    wide_buf,
-    left_send,
-    right_send,
-    pair_bufs,
-    core_bufs,
-    xbuf,
-    xrecv,
-    send_sem,
-    recv_sem,
-    io_sem,
-    ready_sem,
-):
+def span(offset, size):
+    return min(offset, size - offset)
+
+
+PANEL_WALK = sorted(
+    ((dz, dy, dx) for dz in range(8) for dy in range(8) for dx in range(2)),
+    key=lambda o: (-span(o[0], 8) - span(o[1], 8), -o[2], (3 * o[0] + 5 * o[1]) % 8),
+)
+CELL_WALKS = (
+    PANEL_WALK,
+    sorted(
+        ((dz, dy, dx) for dz in range(4) for dy in range(8) for dx in range(4)),
+        key=lambda o: (-2 * span(o[0], 4) - span(o[1], 8) - span(o[2], 4), (3 * o[0] + 5 * o[1]) % 8),
+    ),
+)
+
+
+def evoformer_kernel(*refs):
+    sources, refs = refs[:13], refs[13:]
+    out_ref, loaded, refs = refs[0], refs[1:14], refs[14:]
+    (
+        row_mask_ref,
+        hidden_gain_ref,
+        hidden_shift_ref,
+        pair_buf,
+        col_mask_ref,
+        pair_gain_ref,
+        pair_shift_ref,
+        panel_weight_ref,
+        panel_bias_ref,
+        gate_weight_ref,
+        gate_bias_ref,
+        output_weight_ref,
+        output_bias_ref,
+    ) = loaded
+    (
+        weight_buf,
+        bias_buf,
+        normed_buf,
+        gate_buf,
+        wide_buf,
+        left_send,
+        right_send,
+        pair_bufs,
+        core_bufs,
+        total_buf,
+        xbuf,
+        xrecv,
+        send_sem,
+        recv_sem,
+        io_sem,
+        ready_sem,
+    ) = refs
     row = lax.axis_index("row")
     ch = lax.axis_index("ch")
     z, y_lo, x = row // 8, (row // 4) % 2, row % 4
@@ -69,8 +84,6 @@
     own_h = z * 16 + y * 2 + hx
 
     barrier = pltpu.get_barrier_semaphore()
-    load = pltpu.make_async_copy(pair_ref, pair_buf, io_sem.at[0])
-    load.start()
 
     def column(t):
         spot = (y_lo * CHANNELS + ch + t) % 16
@@ -89,6 +102,14 @@
 
     signals(barrier, plane, 32)
     signals(barrier, column, 16)
+    loads = [
+        pltpu.make_async_copy(source, ref, io_sem.at[4 + i])
+        for i, (source, ref) in enumerate(zip(sources, loaded))
+    ]
+    for load in loads:
+        load.start()
+    for load in loads:
+        load.wait()
 
     col_mask = col_mask_ref[pl.ds(ch, 1), :].astype(jnp.float32)
 
@@ -188,7 +209,7 @@
 
     def store(part):
         some = pl.ds(part * 4, 4)
-        return pltpu.make_async_copy(pair_buf.at[some], out_ref.at[some], io_sem.at[1 + part])
+        return pltpu.make_async_copy(pair_buf.at[some], out_ref.at[some], io_sem.at[part])
 
     def remote(src, dst, sent, got, there):
         return pltpu.make_async_remote_copy(
@@ -223,27 +244,23 @@
                 pltpu.make_async_copy(one, one, send_sem.at[sent + 1]).wait
             )
 
-    def target(t, to_half, to_core):
-        dz, dy, dx = shuffled(t)
-        z_t, y_t, hx_t = (z + dz) % 8, (y + dy) % 8, (hx + dx) % 2
-        x_t = hx_t + to_half * (3 - 2 * hx_t)
-        there = {"row": z_t * 8 + (y_t % 2) * 4 + x_t, "ch": (y_t // 2) * 2 + to_core}
-        return z_t * 16 + y_t * 2 + hx_t, there
-
-    def panel_sends(ref, slot, to_half, to_core, sent, gots, to_self):
-        h_0, there_0 = target(0, to_half, to_core)
-        first(ref.at[h_0], slot, sent + 1, gots[0], there_0, to_self)
-
-        def sends(got):
-            def body(t, carry):
-                h_t, there = target(t, to_half, to_core)
-                remote(ref.at[h_t], slot, sent, got, there).start()
-                return carry
-
-            return body
-
-        lax.fori_loop(1, 64, sends(gots[0]), 0)
-        lax.fori_loop(64, HIDDEN, sends(gots[1]), 0)
+    zs = [(z + d) % 8 for d in range(8)]
+    ys = [(y + d) % 8 for d in range(8)]
+    y_rows = [(y_t % 2) * 4 for y_t in ys]
+    y_chs = [(y_t // 2) * 2 for y_t in ys]
+
+    def panel_sends(ref, slot, to_half, to_core, sent, gots, to_self, dxs):
+        hs = [(hx + d) % 2 for d in range(2)]
+        xs = [hx_t + to_half * (3 - 2 * hx_t) for hx_t in hs]
+        for dz, dy, dx in PANEL_WALK:
+            if dx not in dxs:
+                continue
+            src = ref.at[zs[dz] * 16 + ys[dy] * 2 + hs[dx]]
+            there = {"row": zs[dz] * 8 + y_rows[dy] + xs[dx], "ch": y_chs[dy] + to_core}
+            if (dz, dy, dx) == (0, 0, 0):
+                first(src, slot, sent + 1, gots[0], there, to_self)
+            else:
+                remote(src, slot, sent, gots[dx], there).start()
 
     partner = {"row": row + 3 - 2 * x, "ch": ch}
     sibling = {"row": row, "ch": ch + 1 - 2 * core}
@@ -261,26 +278,27 @@
             pair_self, core_self, x_self = core == z % 2, None, None
         else:
             pair_base, core_base = 0, 2 * HIDDEN
-            block = pl.ds(((y_hi % 2) * 2 + core) * LANE, LANE)
-            pair_slot = pair_panel.at[z // 4, z % 4, y_lo, x_hi, rows, block]
+            pair_slot = pair_panel.at[z // 4, z % 4, y_lo, x_hi, rows, lanes]
             core_slot = core_panel.at[z // 4, pl.ds((row % 32) * TILE, TILE), lanes]
-            pair_to, core_to = (x_hi, y_hi // 2), (core, z // 4)
-            pair_self = core == y_hi // 2
-            core_self = x_self = jnp.logical_and(core == z // 4, core == x_hi)
+            pair_to, core_to = (x_hi, core), (core, z // 4)
+            pair_self = None
+            core_self = jnp.logical_and(core == z // 4, core == x_hi)
+            x_self = jnp.logical_and(core == z % 2, core == x_hi)
 
         normalize(section)
         if section == 0:
             pl.semaphore_wait(barrier, 46)
-            signals(ready_sem, plane, 32)
+            signals(ready_sem, column, 16)
         panel(section, pair_base, right_send)
         if section == 0:
-            pl.semaphore_wait(ready_sem, 31)
-        panel_sends(right_send, pair_slot, *pair_to, s, (g, g + 1), pair_self)
+            pl.semaphore_wait(ready_sem, 15)
+        panel_sends(right_send, pair_slot, *pair_to, s, (g, g + 1), pair_self, (1,))
+        panel_sends(right_send, pair_slot, *pair_to, s, (g, g + 1), pair_self, (0,))
         panel(section, core_base, left_send)
-        panel_sends(left_send, core_slot, *core_to, s + 2, (g + 2, g + 2), core_self)
+        panel_sends(left_send, core_slot, *core_to, s + 2, (g + 2, g + 2), core_self, (0, 1))
         gate(section)
 
-        for dx in range(2):
+        for dx in (1, 0):
             tiles = left_send.at[pl.ds(0, HIDDEN // 2)]
             pltpu.make_async_copy(tiles, tiles, recv_sem.at[g + dx]).wait()
             hx_s = (hx + dx) % 2
@@ -293,54 +311,46 @@
         got_all(g + 2)
         remote(core_panel.at[core], core_panel.at[core], s + 5, g + 4, sibling).start()
         got_all(g + 3)
-        got_all(g + 4)
-
-        if section == 0:
-            products = None
-            for part in range(2):
-                term = lax.dot_general(
+
+        def term(part):
+            if section == 0:
+                return lax.dot_general(
                     core_bufs[section, part],
                     pair_bufs[section, part].reshape(512, 512),
                     (((1,), (1,)), ((), ())),
                     preferred_element_type=jnp.float32,
                 )
-                products = term if products is None else products + term
-        else:
-            products = lax.dot_general(
-                pair_bufs[section].reshape(1024, 512),
-                core_bufs[section].reshape(1024, 512),
+            return lax.dot_general(
+                pair_bufs[section, part].reshape(512, 512),
+                core_bufs[section, part],
                 (((0,), (0,)), ((), ())),
                 preferred_element_type=jnp.float32,
             )
-        xbuf[section] = products.astype(jnp.bfloat16)
-
-        def cell(t):
-            dz, dy, dx = shuffled(t)
-            y_t = (y + dy) % 8
+
+        total_buf[...] = term(core)
+        got_all(g + 4)
+        xbuf[section] = (total_buf[...] + term(1 - core)).astype(jnp.bfloat16)
+
+        x_slot = xrecv.at[section, own_h]
+        odd = (z + core) % 2
+        returns = zs if section == 0 else [(z + odd + 2 * d) % 8 for d in range(4)]
+        lows = [(x_lo + d) % 2 for d in range(2)]
+        xs = [half * 2 + low_t for low_t in lows] if section == 0 else [(x + d) % 4 for d in range(4)]
+        for dz, dy, dx in CELL_WALKS[section]:
+            z_t, x_t = returns[dz], xs[dx]
             if section == 0:
-                z_t, low_t = (z + dz) % 8, (x_lo + dx) % 2
-                block = z_t * 4 + (y_t % 2) * 2 + low_t
-                row_t = z_t * 8 + (y_t % 2) * 4 + half * 2 + low_t
-                core_t = core
+                block = z_t * 4 + (ys[dy] % 2) * 2 + lows[dx]
             else:
-                q_t = (z + dz % 4) % 4
-                x_t = (x + (dz // 4) * 2 + dx) % 4
-                block = q_t * 8 + (y_t % 2) * 4 + x_t
-                row_t = core * 32 + block
-                core_t = half
-            src = xbuf.at[section, pl.ds(block * TILE, TILE), pl.ds((y_t // 2) * LANE, LANE)]
-            return src, {"row": row_t, "ch": (y_t // 2) * 2 + core_t}
-
-        x_slot = xrecv.at[section, own_h]
-        src_0, there_0 = cell(0)
-        first(src_0, x_slot, s + 7, g + 5, there_0, x_self)
-
-        def body(t, carry):
-            src, there = cell(t)
-            remote(src, x_slot, s + 6, g + 5, there).start()
-            return carry
-
-        lax.fori_loop(1, HIDDEN, body, 0)
+                block = (z_t // 2) * 8 + y_rows[dy] + x_t
+            src = xbuf.at[section, pl.ds(block * TILE, TILE), pl.ds((ys[dy] // 2) * LANE, LANE)]
+            there = {
+                "row": z_t * 8 + y_rows[dy] + x_t,
+                "ch": y_chs[dy] + (core if section == 0 else half),
+            }
+            if (dz, dy, dx) == (0, 0, 0):
+                first(src, x_slot, s + 7, g + 5, there, x_self)
+            else:
+                remote(src, x_slot, s + 6, g + 5, there).start()
         sent_rest(s, pair_self)
         sent_rest(s + 2, core_self)
         sent_all(s + 4)
@@ -351,7 +361,6 @@
 
     prepare(0)
     prepare(1)
-    load.wait()
     update(0)
     update(1)
     for part in range(4):
@@ -372,35 +381,8 @@
     output_weight,
     output_bias,
 ):
-    smem = pl.BlockSpec(memory_space=pltpu.SMEM)
-    vmem = pl.BlockSpec(memory_space=pltpu.VMEM)
     half = jnp.bfloat16
-    return pl.pallas_call(
-        evoformer_kernel,
-        out_shape=jax.ShapeDtypeStruct(pair_rep.shape, jnp.float32),
-        in_specs=[smem] * 3 + [pl.BlockSpec(memory_space=pl.ANY)] + [vmem] * 9,
-        out_specs=pl.BlockSpec(memory_space=pl.ANY),
-        scratch_shapes=[
-            pltpu.VMEM((TILE, LANE, LANE), jnp.float32),
-            pltpu.VMEM((2, 4 * HIDDEN, LANE), half),
-            pltpu.VMEM((2, 4 * HIDDEN, LANE), jnp.float32),
-            pltpu.VMEM((TILE, LANE, LANE), half),
-            pltpu.VMEM((TILE, LANE, LANE), jnp.float32),
-            pltpu.VMEM((HIDDEN * TILE, LANE), jnp.float32),
-            pltpu.VMEM((HIDDEN, TILE, LANE), half),
-            pltpu.VMEM((HIDDEN, TILE, LANE), half),
-            pltpu.VMEM((2, 2, 4, 2, 2, 32, 512), half),
-            pltpu.VMEM((2, 2, 512, 512), half),
-            pltpu.VMEM((2, 512, 512), half),
-            pltpu.VMEM((2, HIDDEN, TILE, LANE), half),
-            pltpu.SemaphoreType.DMA((16,)),
-            pltpu.SemaphoreType.DMA((12,)),
-            pltpu.SemaphoreType.DMA((5,)),
-            pltpu.SemaphoreType.REGULAR,
-        ],
-        compiler_params=pltpu.CompilerParams(collective_id=0, has_side_effects=True),
-        name="evoformer",
-    )(
+    operands = (
         residue_mask,
         hidden_gain,
         hidden_shift,
@@ -415,6 +397,36 @@
         output_weight,
         output_bias,
     )
+    return pl.pallas_call(
+        evoformer_kernel,
+        out_shape=jax.ShapeDtypeStruct(pair_rep.shape, jnp.float32),
+        in_specs=[pl.BlockSpec(memory_space=pltpu.HBM)] * len(operands),
+        out_specs=pl.BlockSpec(memory_space=pl.ANY),
+        scratch_shapes=[
+            *(
+                (pltpu.SMEM if i < 3 else pltpu.VMEM)(operand.shape, operand.dtype)
+                for i, operand in enumerate(operands)
+            ),
+            pltpu.VMEM((2, 4 * HIDDEN, LANE), half),
+            pltpu.VMEM((2, 4 * HIDDEN, LANE), jnp.float32),
+            pltpu.VMEM((TILE, LANE, LANE), half),
+            pltpu.VMEM((TILE, LANE, LANE), jnp.float32),
+            pltpu.VMEM((HIDDEN * TILE, LANE), jnp.float32),
+            pltpu.VMEM((HIDDEN, TILE, LANE), half),
+            pltpu.VMEM((HIDDEN, TILE, LANE), half),
+            pltpu.VMEM((2, 2, 4, 2, 2, 32, 512), half),
+            pltpu.VMEM((2, 2, 512, 512), half),
+            pltpu.VMEM((512, 512), jnp.float32),
+            pltpu.VMEM((2, 512, 512), half),
+            pltpu.VMEM((2, HIDDEN, TILE, LANE), half),
+            pltpu.SemaphoreType.DMA((16,)),
+            pltpu.SemaphoreType.DMA((12,)),
+            pltpu.SemaphoreType.DMA((4 + len(operands),)),
+            pltpu.SemaphoreType.REGULAR,
+        ],
+        compiler_params=pltpu.CompilerParams(collective_id=0, has_side_effects=True),
+        name="evoformer",
+    )(*operands)
 
 
 def solution(mesh):

time: 127 us -> 117 us (0.921)
  Pallas kernels: 125 us -> 115 us
    pallas_call x1, Pallas kernels: 125 us -> 115 us  [local(): pl.pallas_call(evoformer_kernel, out_shape=jax.ShapeDtypeStruct(pair_rep....]
where the time goes in v4:
time: 117 us
  Pallas kernels  115 us (98%)
  local copies, waits for them, and re-layouts  2.3 us (2%)
    pallas_call x1, Pallas kernels, local(): pl.pallas_call(evoformer_kernel, out_shape=jax.ShapeDtypeStruct(pair_rep....  115 us

profile of v4, /device:TPU:1, one launch (start us, length us, event | category | flops | bytes accessed | tf_op | source)
XLA Modules:
  0.0 116.8 jit_solution(15643088504971002037)
XLA Ops:
  0.0 114.5 %evoformer.1 = f32[16,128,128]{2,1,0:T(8,128)} custom-call(s32[1024]{0:T(1024)} %refs_0_.1, f32[2,128]{1,0:T(2,128)} %refs_1_.1, f32[2,128]{1,0:T(2,128)} %refs_2_.1, f32[16,128,128]{2,1,0:T(8,128)} %refs_3_.1, s32[8,128]{1,0:T(8,128)} %bitcast.1, f32[2,128]{1,0:T(2,128)} %refs_5_.1, f32[2,128]{1,0:T(2,128)} %refs_6_.1, bf16[2,128,512]{2,1,0:T(8,128)(2,1)} %refs_7_.1, ...), custom_call_target="tpu_custom_call" | custom-call | tf_op jit(solution)/shard_map/evoformer/pallas_call | solution.py:400
  114.5 2.3 %copy.14 = f32[16,128,128]{2,1,0:T(8,128)} copy(f32[16,128,128]{2,1,0:T(8,128)} %evoformer.1) | data formatting | bytes 2097152

commit v5 on v4

--- a/solution.py
+++ b/solution.py
@@ -85,23 +85,26 @@
 
     barrier = pltpu.get_barrier_semaphore()
 
-    def column(t):
-        spot = (y_lo * CHANNELS + ch + t) % 16
-        return {"row": z * 8 + (spot // CHANNELS) * 4 + x, "ch": spot % CHANNELS}
-
-    def plane(t):
-        spot = (z * 4 + x + t) % 32
-        return {"row": (spot // 4) * 8 + y_lo * 4 + spot % 4, "ch": ch}
-
-    def signals(sem, group, count):
-        def body(t, carry):
-            pl.semaphore_signal(sem, inc=1, device_id=group(t), device_id_type=MESH)
-            return carry
-
-        lax.fori_loop(1, count, body, 0)
-
-    signals(barrier, plane, 32)
-    signals(barrier, column, 16)
+    def signals(sem, spots):
+        for there in spots:
+            pl.semaphore_signal(sem, inc=1, device_id=there, device_id_type=MESH)
+
+    plane = [
+        {"row": ((z + dz) % 8) * 8 + y_lo * 4 + (x + dx) % 4, "ch": ch}
+        for dz, dx in sorted(
+            ((dz, dx) for dz in range(8) for dx in range(4)),
+            key=lambda o: -span(o[0], 8) - span(o[1], 4),
+        )[:-1]
+    ]
+    column = [
+        {"row": z * 8 + ((y_lo + dl) % 2) * 4 + x, "ch": (ch + dc) % CHANNELS}
+        for dc, dl in sorted(
+            ((dc, dl) for dc in range(8) for dl in range(2)),
+            key=lambda o: -span(o[0], 8) - o[1],
+        )[:-1]
+    ]
+    signals(barrier, plane)
+    signals(barrier, column)
     loads = [
         pltpu.make_async_copy(source, ref, io_sem.at[4 + i])
         for i, (source, ref) in enumerate(zip(sources, loaded))
@@ -288,7 +291,7 @@
         normalize(section)
         if section == 0:
             pl.semaphore_wait(barrier, 46)
-            signals(ready_sem, column, 16)
+            signals(ready_sem, column)
         panel(section, pair_base, right_send)
         if section == 0:
             pl.semaphore_wait(ready_sem, 15)

time: 117 us -> 116 us (level)
  no operation moved by 1% of the time
where the time goes in v5:
time: 116 us
  Pallas kernels  114 us (98%)
  local copies, waits for them, and re-layouts  2.3 us (2%)
    pallas_call x1, Pallas kernels, local(): pl.pallas_call(evoformer_kernel, out_shape=jax.ShapeDtypeStruct(pair_rep....  114 us

profile of v5, /device:TPU:1, one launch (start us, length us, event | category | flops | bytes accessed | tf_op | source)
XLA Modules:
  0.0 116.2 jit_solution(15296225165140355344)
XLA Ops:
  0.0 113.9 %evoformer.1 = f32[16,128,128]{2,1,0:T(8,128)} custom-call(s32[1024]{0:T(1024)} %refs_0_.1, f32[2,128]{1,0:T(2,128)} %refs_1_.1, f32[2,128]{1,0:T(2,128)} %refs_2_.1, f32[16,128,128]{2,1,0:T(8,128)} %refs_3_.1, s32[8,128]{1,0:T(8,128)} %bitcast.1, f32[2,128]{1,0:T(2,128)} %refs_5_.1, f32[2,128]{1,0:T(2,128)} %refs_6_.1, bf16[2,128,512]{2,1,0:T(8,128)(2,1)} %refs_7_.1, ...), custom_call_target="tpu_custom_call" | custom-call | tf_op jit(solution)/shard_map/evoformer/pallas_call | solution.py:403
  113.9 2.3 %copy.14 = f32[16,128,128]{2,1,0:T(8,128)} copy(f32[16,128,128]{2,1,0:T(8,128)} %evoformer.1) | data formatting | bytes 2097152
